TPU v7x, 256 devices: a whole 4x4x8 slice. The times are simulated.
256 devices in a mesh: tab: 16 (over z_lo, x), cand: 4 (over z_hi, core), dp: 4 (over y).
Axes of the slice: x: 4, y: 4, z: 8 (z_hi: 2, z_lo: 4; z = z_hi * 4 + z_lo), core: 2. Of those that a mesh axis runs over, the one named last changes fastest.
Arguments:
- tables: bfloat16 [16, 524288, 128], P(('cand', 'dp'), 'tab'), may hold values from -6 to 6
- bag_ids: int32 [16, 1024, 16], P(('cand', 'dp')), may hold values from 0 to 524287
- bag_lengths: int32 [16, 1024], P(('cand', 'dp')), may hold values from 1 to 16
- item_weight: bfloat16 [2048, 256], replicated, may hold values from -0.125 to 0.125
- user_features: bfloat16 [131072, 512], P(('tab', 'dp')), may hold values from -6 to 6
- user_w1: bfloat16 [512, 1024], replicated, may hold values from -0.25 to 0.25
- user_w2: bfloat16 [1024, 256], replicated, may hold values from -0.1875 to 0.1875
- positive_items: int32 [131072], P(('tab', 'dp')), may hold values from 0 to 1023
Outputs:
- item_emb: float32 [1024, 256], P(('tab', 'cand', 'dp'))
- user_loss: float32 [131072], P(('tab', 'dp'))
Inputs may be any that keep to these rules, and one draw needn't show every extreme that they name: `bag_ids`: row ids of a table. Only the first bag_lengths ids of a bag count; the rest is padding.
All inputs are finite; a program needn't handle non-finite values.
Results may differ from a plain program's by a relative error of at most 0.00046.
Values sent between devices are 32-bit elements; how exact they have to be, the bound alone decides.
A program may use at most 64 MiB of HBM per device.

v0:
```python
import jax
import jax.numpy as jnp
from jax import lax
from jax.sharding import PartitionSpec as P

epsilon = 1e-06
logit_scale = 20.0


def split_up(value, dim, size):
    lengths = value.shape
    parts = value.reshape(*lengths[:dim], size, lengths[dim] // size, *lengths[dim + 1 :])
    return jnp.moveaxis(parts, dim, 0)


def summed_on_arrival(value, axis, dim):
    size = lax.axis_size(axis)
    parts = lax.all_to_all(split_up(value, dim, size), axis, 0, 0, tiled=True)
    return jnp.sum(parts, axis=0)


def in_order(parts, dim):
    parts = jnp.moveaxis(parts, 0, dim)
    lengths = parts.shape
    return parts.reshape(*lengths[:dim], lengths[dim] * lengths[dim + 1], *lengths[dim + 2 :])


def copy_for_each(value, axis):
    copies = jnp.broadcast_to(value, (lax.axis_size(axis), *value.shape))
    return lax.all_to_all(copies, axis, split_axis=0, concat_axis=0, tiled=True)


def gather_directly(value, axis, dim):
    return in_order(copy_for_each(value, axis), dim)


def over_copies(value, axis):
    everything = copy_for_each(value, axis)
    return jnp.sum(everything, axis=0)


def in_one(arrays, axis):
    ends = [0]
    for a in arrays:
        ends.append(ends[-1] + a.size)
    total = over_copies(jnp.concatenate([a.ravel() for a in arrays]), axis)
    return tuple((total[b:e].reshape(a.shape) for a, b, e in zip(arrays, ends, ends[1:])))


def unit_rows(vectors):
    return vectors * lax.rsqrt(jnp.mean(vectors * vectors, axis=-1, keepdims=True) + epsilon)


def lookup_pool(bag_part, length_part, table, row_base):
    rows_total = table.shape[0]
    local = bag_part - row_base
    inside = (local >= 0) & (local < rows_total)
    valid = lax.broadcasted_iota(jnp.int32, bag_part.shape, 1) < length_part[:, None]
    keeping = inside & valid
    picked = jnp.take(table, jnp.clip(local, 0, rows_total - 1), axis=0).astype(jnp.float32)
    summed = jnp.sum(jnp.where(keeping[:, :, None], picked, jnp.float32(0.0)), axis=1)
    return summed / length_part[:, None].astype(jnp.float32)


def user_tower(features, user_w1, user_w2):
    user_hidden = jax.nn.gelu(
        jnp.dot(features, user_w1, preferred_element_type=jnp.float32), approximate=False
    ).astype(jnp.bfloat16)
    return unit_rows(jnp.dot(user_hidden, user_w2, preferred_element_type=jnp.float32))


def body(
    tables, bag_ids, bag_lengths, item_weight, user_features, user_w1, user_w2, positive_items
):
    table = tables[0]
    own_ids = bag_ids[0]
    own_lengths = bag_lengths[0]
    num_cand = lax.axis_size("cand")
    num_dp = lax.axis_size("dp")
    width = table.shape[1]
    embed = item_weight.shape[1]
    table_count = item_weight.shape[0] // width
    row_base = lax.axis_index("tab") * table.shape[0]
    pooled = summed_on_arrival(lookup_pool(own_ids, own_lengths, table, row_base), "tab", 0)
    groups = num_cand * num_dp
    shaped = pooled.reshape(1, groups, pooled.shape[0] // groups, width)
    weight_blocks = item_weight.astype(jnp.float32).reshape(table_count, width, embed)
    stacked = lax.all_to_all(shaped, ("cand", "dp"), split_axis=1, concat_axis=0, tiled=True)[:, 0]
    item_pre = jnp.einsum(
        "fbe,feh->bh",
        stacked,
        weight_blocks,
        precision=lax.Precision.HIGHEST,
        preferred_element_type=jnp.float32,
    )
    item_emb = unit_rows(item_pre)
    scale = logit_scale / embed
    per_block = item_emb.shape[0]
    cand_index = lax.axis_index("cand")

    def make_adder(user_emb, positives):

        def add_scores(carry, piece, global_id):
            scores = (
                lax.dot_general(
                    user_emb,
                    piece,
                    (((1,), (1,)), ((), ())),
                    precision=lax.Precision.HIGHEST,
                    preferred_element_type=jnp.float32,
                )
                * scale
            )
            sums = jnp.sum(jnp.exp(scores), axis=1)
            positive = jnp.sum(
                jnp.where(global_id == positives[:, None], scores, jnp.float32(0.0)), axis=1
            )
            return (sums, positive)

        return add_scores

    user_emb = user_tower(user_features, user_w1, user_w2)
    users_here = user_emb.shape[0]
    start_carry = (jnp.zeros((users_here,), jnp.float32), jnp.zeros((users_here,), jnp.float32))
    add_scores = make_adder(user_emb, positive_items)
    piece = gather_directly(item_emb, ("tab", "dp"), 0)
    place = lax.broadcasted_iota(jnp.int32, (1, piece.shape[0]), 1)
    group = place // per_block
    within = place % per_block
    global_id = (
        (group // num_dp * num_cand + cand_index) * num_dp + group % num_dp
    ) * per_block + within
    partial_sums = add_scores(start_carry, piece, global_id)
    sums, positive = in_one((partial_sums[0], partial_sums[1]), "cand")
    user_loss = jnp.log(sums) - positive
    return (item_emb, user_loss)


def solution(mesh):
    placed = (
        P(("cand", "dp"), "tab", None),
        P(("cand", "dp"), None, None),
        P(("cand", "dp"), None),
        P(),
        P(("tab", "dp"), None),
        P(),
        P(),
        P(("tab", "dp")),
    )
    return jax.shard_map(
        body,
        mesh=mesh,
        in_specs=placed,
        out_specs=(P(("tab", "cand", "dp"), None), P(("tab", "dp"))),
        check_vma=False,
    )
```

profile of v0, /device:TPU:1, one launch (start us, length us, event | category | flops | bytes accessed | tf_op | source)
XLA Modules:
  0.0 161.8 jit_solution(17984595287167455279)
XLA Ops:
  0.6 0.0 copy-start
  0.7 0.8 convert_reduce_fusion
  1.5 0.9 compare_select_fusion
  2.4 0.9 fusion.16
  3.3 0.3 copy.22
  3.5 0.3 copy.23
  3.8 0.2 copy.24
  4.0 0.2 reshape.243
  4.2 0.1 convert_element_type.20
  4.3 59.4 %gather_fusion = bf16[16384,128]{1,0:T(8,128)(2,1)} fusion(bf16[32768,128]{1,0:T(8,128)(2,1)} %bitcast.31, s32[16384]{0:T(1024)S(1)} %broadcast_clamp_fusion), kind=kCustom, calls=%fused_computation | custom fusion | bytes 8454144 | tf_op jit(solution)/shard_map/jit(_take)/gather | solution.py:60
  63.7 0.0 copy-start.2
  63.7 7.3 %select_reduce_fusion = f32[1024,128]{1,0:T(8,128)S(1)} fusion(pred[1024,16]{1,0:T(8,128)(4,1)S(1)} %copy.23, pred[1024,16]{1,0:T(8,128)(4,1)S(1)} %copy.22, bf16[16384,128]{1,0:T(8,128)(2,1)} %gather_fusion), kind=kLoop, calls=%fused_computation.18 | loop fusion | flops 8257536 | bytes 4751360 | tf_op jit(solution)/shard_map/reduce_sum | solution.py:61
  71.0 0.2 broadcast_divide_fusion
  71.2 22.6 %all_to_all.25 = f32[16,64,128]{2,1,0:T(8,128)S(1)} all-to-all(f32[16,64,128]{2,1,0:T(8,128)S(1)} %broadcast_divide_fusion), channel_id=1, replica_groups=mesh['tab'=16,'cand'=4,'dp'=4] {'tab'}, dimensions={0} | all-to-all | bytes 1048576 | tf_op jit(solution)/shard_map/all_to_all | solution.py:18
  93.8 20.4 %all_to_all.26 = f32[1,16,4,128]{3,2,0,1:T(4,128)S(1)} all-to-all(f32[1,16,4,128]{3,2,0,1:T(4,128)S(1)} %bitcast.34), channel_id=1, replica_groups=mesh['tab'=16,'cand'=4,'dp'=4] {'cand','dp'}, dimensions={1} | all-to-all | bytes 65536 | tf_op jit(solution)/shard_map/all_to_all | solution.py:88
  114.2 1.9 %multiply_reduce_fusion.1 = (f32[4]{0:T(128)S(1)}, f32[4,256]{1,0:T(4,128)S(1)}) fusion(bf16[16,128,256]{2,1,0:T(8,128)(2,1)} %bitcast.33, f32[1,16,4,128]{3,2,0,1:T(4,128)S(1)} %all_to_all.26), kind=kOutput, calls=%fused_computation.42 | convolution fusion | flops 25167868 | bytes 1085456 | tf_op jit(solution)/shard_map/fbe,feh->bh/dot_general | solution.py:89
  116.1 0.1 broadcast_multiply_fusion
  116.2 0.0 copy-start.1
  116.2 0.8 broadcast_in_dim.40
  116.9 6.0 %all-to-all-start.2 = ((f32[64,4,256]{2,1,0:T(4,128)}), f32[64,4,256]{2,1,0:T(4,128)S(1)}, u32[]{:S(2)}, u32[]{:S(2)}) async-start(f32[64,4,256]{2,1,0:T(4,128)} %broadcast_in_dim.40), calls=%async_computation.2 | async-start | bytes 524288 | tf_op jit(solution)/shard_map/all_to_all | solution.py:30
  123.0 0.0 copy-done
  123.0 0.0 copy-done.2
  123.0 0.0 copy-start.3
  123.0 23.0 %multiply_reduce_fusion = (f32[2048]{0:T(1024)S(1)}, f32[2048,256]{0,1:T(8,128)}) fusion(bf16[1024,256]{1,0:T(8,128)(2,1)S(1)} %copy-done.2, bf16[2048,512]{1,0:T(8,128)(2,1)S(1)} %copy-done, bf16[512,1024]{1,0:T(8,128)(2,1)} %param.13), kind=kOutput, calls=%fused_computation.27 | convolution fusion | flops 3358586880 | bytes 5775360 | tf_op jit(solution)/shard_map/dot_general | solution.py:69
  146.0 0.0 copy-done.1
  146.0 0.0 all-to-all-done.2
  146.0 0.1 reshape.240
  146.1 0.0 copy-done.3
  146.1 4.1 %exponential_reduce_fusion = (f32[2048]{0:T(1024)S(1)}, f32[2048]{0:T(1024)S(1)}) fusion(s32[2048]{0:T(1024)S(1)} %copy-done.3, s32[256]{0:T(256)S(1)} %fusion.20, f32[256,256]{1,0:T(8,128)S(1)} %reshape.240, f32[2048,256]{0,1:T(8,128)} %get-tuple-element.9, f32[2048]{0:T(1024)S(1)} %add_rsqrt_fusion), kind=kOutput, calls=%fused_computation.25 | convolution fusion | flops 1613754368 | bytes 2393088 | tf_op jit(solution)/shard_map/dot_general | solution.py:105
  150.3 10.9 %all_to_all.27 = f32[4,1,4096]{2,1,0:T(1,128)S(1)} all-to-all(f32[4,1,4096]{2,1,0:T(1,128)S(1)} %broadcast_in_dim.42), channel_id=1, replica_groups=mesh['tab'=16,'cand'=4,'dp'=4] {'cand'}, dimensions={0} | all-to-all | bytes 131072 | tf_op jit(solution)/shard_map/all_to_all | solution.py:30
  161.1 0.1 reduce_sum.72
  161.2 0.6 slice_subtract_fusion
  (7 shorter events, 0.1 us)
Async XLA Ops:
  0.6 122.3 %copy-start = (bf16[2048,512]{1,0:T(8,128)(2,1)S(1)}, bf16[2048,512]{1,0:T(8,128)(2,1)}, u32[]{:S(2)}) copy-start(bf16[2048,512]{1,0:T(8,128)(2,1)} %param.12) | copy-start | bytes 6291460
  63.7 59.3 %copy-start.2 = (bf16[1024,256]{1,0:T(8,128)(2,1)S(1)}, bf16[1024,256]{1,0:T(8,128)(2,1)}, u32[]{:S(2)}) copy-start(bf16[1024,256]{1,0:T(8,128)(2,1)} %param.14) | copy-start | bytes 1572868
  116.2 29.8 %copy-start.1 = (f32[4,256]{1,0:T(4,128)}, f32[4,256]{1,0:T(4,128)S(1)}, u32[]{:S(2)}) copy-start(f32[4,256]{1,0:T(4,128)S(1)} %broadcast_multiply_fusion) | copy-start | bytes 12292
  116.9 29.1 %all-to-all-start.2 = ((f32[64,4,256]{2,1,0:T(4,128)}), f32[64,4,256]{2,1,0:T(4,128)S(1)}, u32[]{:S(2)}, u32[]{:S(2)}) async-start(f32[64,4,256]{2,1,0:T(4,128)} %broadcast_in_dim.40), calls=%async_computation.2 | async-start | bytes 524288 | tf_op jit(solution)/shard_map/all_to_all | solution.py:30
  123.0 23.2 %copy-start.3 = (s32[2048]{0:T(1024)S(1)}, s32[2048]{0:T(1024)}, u32[]{:S(2)}) copy-start(s32[2048]{0:T(1024)} %param.15) | copy-start | bytes 24580
where the time goes:
time: 162 us
  local copies, waits for them, and re-layouts  61.3 us (38%)
  blocking collectives  53.9 us (33%)
  matrix products  28.9 us (18%)
  other arithmetic  10.9 us (7%)
  starting transfers between devices  6.02 us (4%)
    gather x1, local copies, waits for them, and re-layouts, lookup_pool(): jnp.take(table, jnp.clip(local, 0, rows_total - 1), axis=0)  59.4 us
    dot_general x1, matrix products, user_tower(): jnp.dot(user_hidden, user_w2, preferred_element_type=jnp.float32)  23 us
    all_to_all x1, blocking collectives, summed_on_arrival(): parts = lax.all_to_all(split_up(value, dim, size), axis, 0, 0, tiled=True)  22.6 us
    all_to_all x1, blocking collectives, body(): lax.all_to_all(shaped, ('cand', 'dp'), split_axis=1, concat_axis=0, tiled...  20.4 us
    all_to_all x1, blocking collectives, copy_for_each(): return lax.all_to_all(copies, axis, split_axis=0, concat_axis=0, tiled=True)  10.9 us
    reduce_sum x1, other arithmetic, lookup_pool(): jnp.sum(jnp.where(keeping[:, :, None], picked, jnp.float32(0.0)), axis=1)  7.25 us
    all_to_all x1, starting transfers between devices, copy_for_each(): return lax.all_to_all(copies, axis, split_axis=0, concat_axis=0, tiled=True)  6.02 us
    dot_general x1, matrix products, add_scores(): lax.dot_general(user_emb, piece, (((1,), (1,)), ((), ())), precision=lax....  4.07 us
  transfers between devices with their start and end apart: 1, of which 0 were waited for; matrix products, arithmetic and copies ran while one was open for 14% of the time, Pallas kernels for 0%

commit v1 on v0

--- a/solution.py
+++ b/solution.py
@@ -1,10 +1,155 @@
+import functools
 import jax
 import jax.numpy as jnp
 from jax import lax
+from jax.experimental import pallas as pl
+from jax.experimental.pallas import tpu as pltpu
 from jax.sharding import PartitionSpec as P
 
+MESH = pl.DeviceIdType.MESH
+f32, bf16, i32 = jnp.float32, jnp.bfloat16, jnp.int32
 epsilon = 1e-06
 logit_scale = 20.0
+NX, NZ = 4, 4
+PARTS = 4
+DEPTH = 16
+CHUNKS = 8
+
+
+def iota(shape, dim):
+    return lax.broadcasted_iota(i32, shape, dim)
+
+
+def pool_kernel(ids_ref, len_ref, table_ref, out_ref, stage, tab, acc0, acc1, acc2, acc3,
+                rank_ref, code_ref, list_ref, slist, load_sems, list_sem):
+    rows = table_ref.shape[0]
+    positions, items = ids_ref.shape
+    tiles = items // 128
+    chunk = rows // CHUNKS
+    base = lax.axis_index("tab") * rows
+    loads = [
+        pltpu.make_async_copy(
+            table_ref.at[pl.ds(c * chunk, chunk)], stage.at[pl.ds(c * chunk, chunk)], load_sems.at[c]
+        )
+        for c in range(CHUNKS)
+    ]
+    for load in loads:
+        load.start()
+    accs = (acc0, acc1, acc2, acc3)
+    dummy = items
+
+    slots = tiles * positions
+    ids = jnp.concatenate([ids_ref[:, 128 * t : 128 * (t + 1)] for t in range(tiles)], axis=0)
+    lengths = jnp.concatenate(
+        [jnp.broadcast_to(len_ref[:, 128 * t : 128 * (t + 1)], (positions, 128)) for t in range(tiles)], axis=0
+    )
+    r = iota((slots, 128), 0)
+    lane = iota((slots, 128), 1)
+    local = ids - base
+    live = (local >= 0) & (local < rows) & (lax.rem(r, positions) < lengths)
+    item = lax.div(r, positions) * 128 + lane
+    per = items // (NX * NZ)
+    block = lax.div(item, per)
+    dest = (lax.rem(block, NX) * NZ + lax.div(block, NX)) * per + lax.rem(item, per)
+    code_ref[...] = local * 2048 + dest
+    livef = jnp.where(live, f32(1.0), f32(0.0)).astype(bf16)
+    below = jnp.where(iota((slots, slots), 0) >= iota((slots, slots), 1), f32(1.0), f32(0.0)).astype(bf16)
+    order = jnp.dot(below, livef, preferred_element_type=f32)
+    rank_ref[...] = jnp.where(live, order - 1.0, f32(-1.0)).astype(i32)
+    counts = order[slots - 1 : slots, :].astype(i32)
+    most = jnp.max(counts)
+
+    for acc in accs:
+        acc[...] = jnp.zeros_like(acc)
+
+    def convert(c):
+        loads[c].wait()
+
+        @pl.loop(0, chunk // 256)
+        def _(s):
+            at = pl.ds(pl.multiple_of(c * chunk + s * 256, 256), 256)
+            tab[at, :] = stage[at, :].astype(f32)
+
+    def make_list(first):
+        for k in range(DEPTH):
+            found = jnp.sum(
+                jnp.where(rank_ref[...] == first + k, code_ref[...], 0), axis=0, keepdims=True
+            )
+            list_ref[k : k + 1, :] = jnp.where(counts > first + k, found, dummy)
+        list_ref[DEPTH : DEPTH + 1, :] = jnp.clip(counts - first, 0, DEPTH)
+
+    def add_listed():
+        @pl.loop(0, 128)
+        def _(at):
+            n = slist[DEPTH, at]
+
+            def group(g, _):
+                for q in range(PARTS):
+                    code = slist[g * PARTS + q, at]
+                    row = lax.shift_right_logical(code, 11)
+                    to = code & 2047
+                    accs[q][pl.ds(to, 1), :] += tab[pl.ds(row, 1), :]
+                return 0
+
+            lax.fori_loop(0, lax.shift_right_logical(n + PARTS - 1, 2), group, 0)
+
+    make_list(0)
+    copy = pltpu.make_async_copy(list_ref, slist, list_sem)
+    copy.start()
+    for c in range(CHUNKS):
+        convert(c)
+    copy.wait()
+    add_listed()
+
+    def more(b, _):
+        make_list(b * DEPTH)
+        copy = pltpu.make_async_copy(list_ref, slist, list_sem)
+        copy.start()
+        copy.wait()
+        add_listed()
+        return 0
+
+    lax.fori_loop(1, lax.div(most + DEPTH - 1, DEPTH), more, 0)
+
+    eye = iota((128, 128), 0) == iota((128, 128), 1)
+    ones = jnp.ones((128, 128), bf16)
+    for b in range(tiles):
+        parts = []
+        for h in range(128 // per):
+            to = b * (128 // per) + h
+            t = (to % NZ) * NX + to // NZ
+            parts.append(len_ref[:, t * per : (t + 1) * per])
+        row = jnp.concatenate(parts, axis=1).astype(f32)
+        spread = jnp.where(eye, jnp.broadcast_to(row, (128, 128)), f32(0.0)).astype(bf16)
+        column = jnp.dot(spread, ones, preferred_element_type=f32)
+        at = pl.ds(128 * b, 128)
+        out_ref[at, :] = (acc0[at, :] + acc1[at, :] + acc2[at, :] + acc3[at, :]) / column
+
+
+def pool(ids_t, lengths, table):
+    rows, width = table.shape
+    positions, items = ids_t.shape
+    slots = positions * items // 128
+    vmem = pl.BlockSpec(memory_space=pltpu.VMEM)
+    return pl.pallas_call(
+        pool_kernel,
+        name="pool",
+        out_shape=jax.ShapeDtypeStruct((items, width), f32),
+        in_specs=[vmem, vmem, pl.BlockSpec(memory_space=pltpu.HBM)],
+        out_specs=vmem,
+        scratch_shapes=[
+            pltpu.VMEM((rows, width), bf16),
+            pltpu.VMEM((rows, width), f32),
+            *[pltpu.VMEM((items + 8, width), f32)] * PARTS,
+            pltpu.VMEM((slots, 128), i32),
+            pltpu.VMEM((slots, 128), i32),
+            pltpu.VMEM((DEPTH + 8, 128), i32),
+            pltpu.SMEM((DEPTH + 8, 128), i32),
+            pltpu.SemaphoreType.DMA((CHUNKS,)),
+            pltpu.SemaphoreType.DMA,
+        ],
+        cost_estimate=pl.CostEstimate(flops=10**8, bytes_accessed=9 * 2**20, transcendentals=0),
+    )(ids_t, lengths, table)
 
 
 def split_up(value, dim, size):
@@ -80,8 +225,10 @@
     width = table.shape[1]
     embed = item_weight.shape[1]
     table_count = item_weight.shape[0] // width
-    row_base = lax.axis_index("tab") * table.shape[0]
-    pooled = summed_on_arrival(lookup_pool(own_ids, own_lengths, table, row_base), "tab", 0)
+    partial = pool(own_ids.T, own_lengths[None, :], table)
+    per = partial.shape[0] // (NX * NZ)
+    partial = partial.reshape(NX, NZ, per, width).transpose(1, 0, 2, 3).reshape(partial.shape)
+    pooled = summed_on_arrival(partial, "tab", 0)
     groups = num_cand * num_dp
     shaped = pooled.reshape(1, groups, pooled.shape[0] // groups, width)
     weight_blocks = item_weight.astype(jnp.float32).reshape(table_count, width, embed)

time: 162 us -> 103 us (0.64)
  local copies, waits for them, and re-layouts: 61.3 us -> 2 us
  Pallas kernels: 0 us -> 10.3 us
  other arithmetic: 10.9 us -> 0.81 us
    gather x1 -> x0, local copies, waits for them, and re-layouts: 59.4 us -> none  [lookup_pool(): jnp.take(table, jnp.clip(local, 0, rows_total - 1), axis=0)]
    pallas_call x0 -> x1, Pallas kernels: none -> 10.3 us  [pool(): pl.pallas_call(pool_kernel, name='pool', out_shape=jax.ShapeDtypeStruct((...]
    reduce_sum x1 -> x0, other arithmetic: 7.25 us -> none  [lookup_pool(): jnp.sum(jnp.where(keeping[:, :, None], picked, jnp.float32(0.0)), axis=1)]
  transfers between devices with their start and end apart: 1 -> 1, of which waited for: 0 -> 0; matrix products, arithmetic and copies ran while one was open for 14% -> 22% of each run, Pallas kernels for 0% -> 0%
where the time goes in v1:
time: 103 us
  blocking collectives  54.1 us (53%)
  matrix products  28.9 us (28%)
  Pallas kernels  10.3 us (10%)
  starting transfers between devices  6.02 us (6%)
  local copies, waits for them, and re-layouts  2 us (2%)
    dot_general x1, matrix products, user_tower(): jnp.dot(user_hidden, user_w2, preferred_element_type=jnp.float32)  23 us
    all_to_all x1, blocking collectives, summed_on_arrival(): parts = lax.all_to_all(split_up(value, dim, size), axis, 0, 0, tiled=True)  22.5 us
    all_to_all x1, blocking collectives, body(): lax.all_to_all(shaped, ('cand', 'dp'), split_axis=1, concat_axis=0, tiled...  20.7 us
    all_to_all x1, blocking collectives, copy_for_each(): return lax.all_to_all(copies, axis, split_axis=0, concat_axis=0, tiled=True)  10.9 us
    pallas_call x1, Pallas kernels, pool(): pl.pallas_call(pool_kernel, name='pool', out_shape=jax.ShapeDtypeStruct((...  10.3 us
    all_to_all x1, starting transfers between devices, copy_for_each(): return lax.all_to_all(copies, axis, split_axis=0, concat_axis=0, tiled=True)  6.02 us
    dot_general x1, matrix products, add_scores(): lax.dot_general(user_emb, piece, (((1,), (1,)), ((), ())), precision=lax....  4.09 us
  transfers between devices with their start and end apart: 1, of which 0 were waited for; matrix products, arithmetic and copies ran while one was open for 22% of the time, Pallas kernels for 0%

profile of v1, /device:TPU:1, one launch (start us, length us, event | category | flops | bytes accessed | tf_op | source)
XLA Modules:
  0.0 102.8 jit_solution(1425642436465408260)
XLA Ops:
  0.6 0.0 copy-start
  0.6 0.0 copy-start.2
  0.7 10.3 %pool.1 = f32[1024,128]{1,0:T(8,128)} custom-call(s32[16,1024]{1,0:T(8,128)} %bitcast.27, s32[1,1024]{1,0:T(1,128)} %len_ref.1, bf16[32768,128]{1,0:T(8,128)(2,1)} %bitcast.22), custom_call_target="tpu_custom_call" | custom-call | flops 100000000 | bytes 9437184 | tf_op jit(solution)/shard_map/pool/pallas_call | solution.py:134
  10.9 1.1 %copy.13 = f32[4,4,64,128]{3,2,0,1:T(8,128)S(1)} copy(f32[4,4,64,128]{3,2,1,0:T(8,128)} %bitcast.23) | data formatting | bytes 1048576 | tf_op jit(solution)/shard_map/reshape | solution.py:230
  12.0 22.5 %all_to_all.25 = f32[16,64,128]{2,1,0:T(8,128)S(1)} all-to-all(f32[16,64,128]{2,1,0:T(8,128)S(1)} %bitcast.24), channel_id=1, replica_groups=mesh['tab'=16,'cand'=4,'dp'=4] {'tab'}, dimensions={0} | all-to-all | bytes 1048576 | tf_op jit(solution)/shard_map/all_to_all | solution.py:163
  34.5 20.7 %all_to_all.26 = f32[1,16,4,128]{3,2,0,1:T(4,128)S(1)} all-to-all(f32[1,16,4,128]{3,2,0,1:T(4,128)S(1)} %bitcast.26), channel_id=1, replica_groups=mesh['tab'=16,'cand'=4,'dp'=4] {'cand','dp'}, dimensions={1} | all-to-all | bytes 65536 | tf_op jit(solution)/shard_map/all_to_all | solution.py:235
  55.2 1.9 %multiply_reduce_fusion.1 = (f32[4]{0:T(128)S(1)}, f32[4,256]{1,0:T(4,128)S(1)}) fusion(bf16[16,128,256]{2,1,0:T(8,128)(2,1)} %bitcast.25, f32[1,16,4,128]{3,2,0,1:T(4,128)S(1)} %all_to_all.26), kind=kOutput, calls=%fused_computation.33 | convolution fusion | flops 25167868 | bytes 1085456 | tf_op jit(solution)/shard_map/fbe,feh->bh/dot_general | solution.py:236
  57.1 0.1 broadcast_multiply_fusion
  57.2 0.0 copy-start.1
  57.2 0.8 broadcast_in_dim.13
  58.0 6.0 %all-to-all-start.2 = ((f32[64,4,256]{2,1,0:T(4,128)}), f32[64,4,256]{2,1,0:T(4,128)S(1)}, u32[]{:S(2)}, u32[]{:S(2)}) async-start(f32[64,4,256]{2,1,0:T(4,128)} %broadcast_in_dim.13), calls=%async_computation.2 | async-start | bytes 524288 | tf_op jit(solution)/shard_map/all_to_all | solution.py:175
  64.0 0.0 copy-done
  64.0 0.0 copy-done.2
  64.0 0.0 copy-start.3
  64.0 23.0 %multiply_reduce_fusion = (f32[2048]{0:T(1024)S(1)}, f32[2048,256]{0,1:T(8,128)}) fusion(bf16[1024,256]{1,0:T(8,128)(2,1)S(1)} %copy-done.2, bf16[2048,512]{1,0:T(8,128)(2,1)S(1)} %copy-done, bf16[512,1024]{1,0:T(8,128)(2,1)} %param.13), kind=kOutput, calls=%fused_computation.25 | convolution fusion | flops 3358586880 | bytes 5775360 | tf_op jit(solution)/shard_map/dot_general | solution.py:214
  87.0 0.0 copy-done.1
  87.0 0.0 all-to-all-done.2
  87.0 0.1 reshape.157
  87.1 0.0 copy-done.3
  87.2 4.1 %exponential_reduce_fusion = (f32[2048]{0:T(1024)S(1)}, f32[2048]{0:T(1024)S(1)}) fusion(s32[2048]{0:T(1024)S(1)} %copy-done.3, s32[256]{0:T(256)S(1)} %fusion.19, f32[256,256]{1,0:T(8,128)S(1)} %reshape.157, f32[2048,256]{0,1:T(8,128)} %get-tuple-element.7, f32[2048]{0:T(1024)S(1)} %add_rsqrt_fusion), kind=kOutput, calls=%fused_computation.23 | convolution fusion | flops 1613754368 | bytes 2393088 | tf_op jit(solution)/shard_map/dot_general | solution.py:252
  91.3 10.9 %all_to_all.27 = f32[4,1,4096]{2,1,0:T(1,128)S(1)} all-to-all(f32[4,1,4096]{2,1,0:T(1,128)S(1)} %broadcast_in_dim.15), channel_id=1, replica_groups=mesh['tab'=16,'cand'=4,'dp'=4] {'cand'}, dimensions={0} | all-to-all | bytes 131072 | tf_op jit(solution)/shard_map/all_to_all | solution.py:175
  102.2 0.1 reduce_sum.59
  102.2 0.6 slice_subtract_fusion
  (6 shorter events, 0.1 us)
Async XLA Ops:
  0.6 63.4 %copy-start = (bf16[2048,512]{1,0:T(8,128)(2,1)S(1)}, bf16[2048,512]{1,0:T(8,128)(2,1)}, u32[]{:S(2)}) copy-start(bf16[2048,512]{1,0:T(8,128)(2,1)} %param.12) | copy-start | bytes 6291460
  0.6 63.3 %copy-start.2 = (bf16[1024,256]{1,0:T(8,128)(2,1)S(1)}, bf16[1024,256]{1,0:T(8,128)(2,1)}, u32[]{:S(2)}) copy-start(bf16[1024,256]{1,0:T(8,128)(2,1)} %param.14) | copy-start | bytes 1572868
  57.2 29.8 %copy-start.1 = (f32[4,256]{1,0:T(4,128)}, f32[4,256]{1,0:T(4,128)S(1)}, u32[]{:S(2)}) copy-start(f32[4,256]{1,0:T(4,128)S(1)} %broadcast_multiply_fusion) | copy-start | bytes 12292
  58.0 29.1 %all-to-all-start.2 = ((f32[64,4,256]{2,1,0:T(4,128)}), f32[64,4,256]{2,1,0:T(4,128)S(1)}, u32[]{:S(2)}, u32[]{:S(2)}) async-start(f32[64,4,256]{2,1,0:T(4,128)} %broadcast_in_dim.13), calls=%async_computation.2 | async-start | bytes 524288 | tf_op jit(solution)/shard_map/all_to_all | solution.py:175
  64.0 23.1 %copy-start.3 = (s32[2048]{0:T(1024)S(1)}, s32[2048]{0:T(1024)}, u32[]{:S(2)}) copy-start(s32[2048]{0:T(1024)} %param.15) | copy-start | bytes 24580

commit v2 on v1

--- a/solution.py
+++ b/solution.py
@@ -152,135 +152,297 @@
     )(ids_t, lengths, table)
 
 
-def split_up(value, dim, size):
-    lengths = value.shape
-    parts = value.reshape(*lengths[:dim], size, lengths[dim] // size, *lengths[dim + 1 :])
-    return jnp.moveaxis(parts, dim, 0)
-
-
-def summed_on_arrival(value, axis, dim):
-    size = lax.axis_size(axis)
-    parts = lax.all_to_all(split_up(value, dim, size), axis, 0, 0, tiled=True)
-    return jnp.sum(parts, axis=0)
-
-
-def in_order(parts, dim):
-    parts = jnp.moveaxis(parts, 0, dim)
-    lengths = parts.shape
-    return parts.reshape(*lengths[:dim], lengths[dim] * lengths[dim + 1], *lengths[dim + 2 :])
-
-
-def copy_for_each(value, axis):
-    copies = jnp.broadcast_to(value, (lax.axis_size(axis), *value.shape))
-    return lax.all_to_all(copies, axis, split_axis=0, concat_axis=0, tiled=True)
-
-
-def gather_directly(value, axis, dim):
-    return in_order(copy_for_each(value, axis), dim)
-
-
-def over_copies(value, axis):
-    everything = copy_for_each(value, axis)
-    return jnp.sum(everything, axis=0)
-
-
-def in_one(arrays, axis):
-    ends = [0]
-    for a in arrays:
-        ends.append(ends[-1] + a.size)
-    total = over_copies(jnp.concatenate([a.ravel() for a in arrays]), axis)
-    return tuple((total[b:e].reshape(a.shape) for a, b, e in zip(arrays, ends, ends[1:])))
-
-
-def unit_rows(vectors):
-    return vectors * lax.rsqrt(jnp.mean(vectors * vectors, axis=-1, keepdims=True) + epsilon)
-
-
-def lookup_pool(bag_part, length_part, table, row_base):
-    rows_total = table.shape[0]
-    local = bag_part - row_base
-    inside = (local >= 0) & (local < rows_total)
-    valid = lax.broadcasted_iota(jnp.int32, bag_part.shape, 1) < length_part[:, None]
-    keeping = inside & valid
-    picked = jnp.take(table, jnp.clip(local, 0, rows_total - 1), axis=0).astype(jnp.float32)
-    summed = jnp.sum(jnp.where(keeping[:, :, None], picked, jnp.float32(0.0)), axis=1)
-    return summed / length_part[:, None].astype(jnp.float32)
-
-
-def user_tower(features, user_w1, user_w2):
-    user_hidden = jax.nn.gelu(
-        jnp.dot(features, user_w1, preferred_element_type=jnp.float32), approximate=False
-    ).astype(jnp.bfloat16)
-    return unit_rows(jnp.dot(user_hidden, user_w2, preferred_element_type=jnp.float32))
+def split2(v):
+    high = v.astype(bf16)
+    return high, (v - high.astype(f32)).astype(bf16)
+
+
+def unit_rows(v):
+    return v * lax.rsqrt(jnp.mean(v * v, axis=-1, keepdims=True) + epsilon)
+
+
+PLAN = (1, 2, 1, 1, 3)
+USERS_AT_ONCE = 256
+
+
+def step_kernel(part_ref, weight_ref, x_ref, w1_ref, w2_ref, place_ref, item_ref, loss_ref,
+                xv, w1v, w2v, wv, high_ref, low_ref, recvx, sendz, recvz, sendt, recvt, embed_ref,
+                gathered, stats, others, load_sems, sx, rx, sz, rz, st, rt, sg, rg, ss, rs):
+    tab, cand, dp = lax.axis_index("tab"), lax.axis_index("cand"), lax.axis_index("dp")
+    xi, zi = lax.rem(tab, NX), lax.div(tab, NX)
+    ntab, ncand, ndp = NX * NZ, 4, 4
+    width = part_ref.shape[1]
+    per = part_ref.shape[0] // ntab
+    groups = ncand * ndp
+    own = per // groups
+    table = cand * ndp + dp
+
+    def local(src, dst, k):
+        copy = pltpu.make_async_copy(src, dst, load_sems.at[k])
+        copy.start()
+        return copy
+
+    loads = [
+        local(x_ref, xv, 0),
+        local(w1_ref, w1v, 1),
+        local(w2_ref, w2v, 2),
+        local(weight_ref.at[pl.ds(pl.multiple_of(table * width, width), width)], wv, 3),
+    ]
+
+    barrier = pltpu.get_barrier_semaphore()
+
+    @pl.loop(1, ntab * ndp)
+    def _(k):
+        peer = lax.rem(tab * ndp + dp + k, ntab * ndp)
+        pl.semaphore_signal(
+            barrier, inc=1, device_id=(lax.div(peer, ndp), cand, lax.rem(peer, ndp)), device_id_type=MESH
+        )
+
+    @pl.loop(ndp, groups)
+    def _(k):
+        peer = lax.rem(cand * ndp + k, groups)
+        pl.semaphore_signal(
+            barrier, inc=1, device_id=(tab, lax.div(peer, ndp), lax.rem(peer, ndp)), device_id_type=MESH
+        )
+
+    done = [0]
+
+    def tower(chunks):
+        if done[0] == 0:
+            for k in range(3):
+                loads[k].wait()
+        first = done[0]
+        done[0] += chunks
+
+        @pl.loop(first, first + chunks)
+        def _(c):
+            at = pl.ds(pl.multiple_of(c * USERS_AT_ONCE, USERS_AT_ONCE), USERS_AT_ONCE)
+            hidden = jnp.dot(xv[at, :], w1v[...], preferred_element_type=f32)
+            hidden = (0.5 * hidden * (1.0 + lax.erf(hidden * f32(0.5**0.5)))).astype(bf16)
+            users = unit_rows(jnp.dot(hidden, w2v[...], preferred_element_type=f32))
+            high, low = split2(users * (logit_scale / users.shape[1]))
+            high_ref[at, :] = high
+            low_ref[at, :] = low
+
+    tower(PLAN[0])
+    pl.semaphore_wait(barrier, ntab * ndp - 1 + groups - ndp)
+
+    xcopies = []
+    turns = (2, 1, 3, 0)
+    for n, k in enumerate(turns):
+        zp = lax.rem(zi + k, NZ)
+        row = []
+        for o in range(1, NX):
+            xp = lax.rem(xi + o, NX)
+            src = part_ref.at[pl.ds(pl.multiple_of((xp * NZ + zp) * per, per), per)]
+            copy = pltpu.make_async_remote_copy(
+                src_ref=src,
+                dst_ref=recvx.at[n, o - 1],
+                send_sem=sx.at[n, o - 1],
+                recv_sem=rx.at[n, o - 1],
+                device_id=(zi * NX + xp, cand, dp),
+                device_id_type=MESH,
+            )
+            copy.start()
+            row.append(copy)
+        xcopies.append(row)
+
+    tower(PLAN[1])
+
+    zcopies = []
+    pooled = None
+    for n, k in enumerate(turns):
+        zp = lax.rem(zi + k, NZ)
+        for copy in xcopies[n]:
+            copy.wait_recv()
+        mine = part_ref[pl.ds(pl.multiple_of((xi * NZ + zp) * per, per), per), :]
+        total = mine + recvx[n, 0] + recvx[n, 1] + recvx[n, 2]
+        if k == 0:
+            pooled = total
+        else:
+            sendz[k - 1] = total
+            copy = pltpu.make_async_remote_copy(
+                src_ref=sendz.at[k - 1],
+                dst_ref=recvz.at[k - 1],
+                send_sem=sz.at[k - 1],
+                recv_sem=rz.at[k - 1],
+                device_id=(zp * NX + xi, cand, dp),
+                device_id_type=MESH,
+            )
+            copy.start()
+            zcopies.append(copy)
+    tower(PLAN[2])
+    loads[3].wait()
+    for copy in zcopies:
+        copy.wait_recv()
+    pooled = pooled + recvz[0] + recvz[1] + recvz[2]
+
+    p0 = pooled.astype(bf16)
+    rest = pooled - p0.astype(f32)
+    p1 = rest.astype(bf16)
+    p2 = (rest - p1.astype(f32)).astype(bf16)
+    terms = jnp.dot(jnp.concatenate([p0, p1, p2], axis=0), wv[...], preferred_element_type=f32)
+    terms = terms[:per] + terms[per : 2 * per] + terms[2 * per :]
+    for b in range(groups):
+        sendt[b] = terms[b * own : (b + 1) * own, :]
+
+    @pl.loop(1, groups)
+    def _(k):
+        peer = lax.rem(table + k, groups)
+        pltpu.make_async_remote_copy(
+            src_ref=sendt.at[peer],
+            dst_ref=recvt.at[k - 1],
+            send_sem=st,
+            recv_sem=rt,
+            device_id=(tab, lax.div(peer, ndp), lax.rem(peer, ndp)),
+            device_id_type=MESH,
+        ).start()
+
+    tower(PLAN[3])
+    all_t = pltpu.make_async_copy(recvt, recvt, rt)
+    all_t.wait()
+    total = sendt[table]
+    for b in range(groups - 1):
+        total = total + recvt[b]
+    embed = unit_rows(total)
+    embed_ref[...] = embed
+    item_ref[...] = embed
+
+    me = tab * ndp + dp
+
+    @pl.loop(1, ntab * ndp)
+    def _(k):
+        peer = lax.rem(me + k, ntab * ndp)
+        pltpu.make_async_remote_copy(
+            src_ref=embed_ref,
+            dst_ref=gathered.at[me],
+            send_sem=sg,
+            recv_sem=rg,
+            device_id=(lax.div(peer, ndp), cand, lax.rem(peer, ndp)),
+            device_id_type=MESH,
+        ).start()
+
+    gathered[me] = embed
+    tower(PLAN[4])
+    most = gathered.at[pl.ds(0, ntab * ndp - 1)]
+    pltpu.make_async_copy(most, most, rg).wait()
+
+    pieces = [gathered[b] for b in range(ntab * ndp)]
+    items = jnp.concatenate(pieces, axis=0)
+    item_high, item_low = split2(items)
+    dims = (((1,), (1,)), ((), ()))
+    count = items.shape[0]
+
+    def score(c, _):
+        at = pl.ds(pl.multiple_of(c * USERS_AT_ONCE, USERS_AT_ONCE), USERS_AT_ONCE)
+        high = high_ref[at, :]
+        scores = (
+            lax.dot_general(item_high, high, dims, preferred_element_type=f32)
+            + lax.dot_general(item_low, high, dims, preferred_element_type=f32)
+            + lax.dot_general(item_high, low_ref[at, :], dims, preferred_element_type=f32)
+        )
+        sums = jnp.sum(jnp.exp(scores), axis=0, keepdims=True)
+        for h in range(USERS_AT_ONCE // 128):
+            line = c * (USERS_AT_ONCE // 128) + h
+            place = place_ref[pl.ds(line, 1), :]
+            block = lax.shift_right_logical(place, 4)
+            here = lax.rem(block, ncand) == cand
+            row = jnp.where(here, lax.div(block, ncand) * 16 + (place & 15), -1)
+            part = scores[:, h * 128 : (h + 1) * 128]
+            positive = jnp.sum(
+                jnp.where(iota((count, 128), 0) == row, part, f32(0.0)), axis=0, keepdims=True
+            )
+            stats[pl.ds(line, 1), :] = sums[:, h * 128 : (h + 1) * 128]
+            stats[pl.ds(line + place_ref.shape[0], 1), :] = positive
+        return 0
+
+    lax.fori_loop(0, xv.shape[0] // USERS_AT_ONCE, score, 0)
+
+    scopies = []
+    for o in range(1, ncand):
+        copy = pltpu.make_async_remote_copy(
+            src_ref=stats,
+            dst_ref=others.at[o - 1],
+            send_sem=ss.at[o - 1],
+            recv_sem=rs.at[o - 1],
+            device_id=(tab, lax.rem(cand + o, ncand), dp),
+            device_id_type=MESH,
+        )
+        copy.start()
+        scopies.append(copy)
+    for row in xcopies:
+        for copy in row:
+            copy.wait_send()
+    for copy in zcopies:
+        copy.wait_send()
+    pltpu.make_async_copy(recvt, recvt, st).wait()
+    pltpu.make_async_copy(most, most, sg).wait()
+    for copy in scopies:
+        copy.wait_recv()
+    both = stats[...] + others[0] + others[1] + others[2]
+    lines = place_ref.shape[0]
+    loss_ref[...] = jnp.log(both[:lines]) - both[lines:]
+    for copy in scopies:
+        copy.wait_send()
+
+
+def step(partial, item_weight, features, user_w1, user_w2, places):
+    items, width = partial.shape
+    users, features_in = features.shape
+    hidden, embed = user_w2.shape
+    per = items // (NX * NZ)
+    own = per // 16
+    lines = users // 128
+    vmem = pl.BlockSpec(memory_space=pltpu.VMEM)
+    hbm = pl.BlockSpec(memory_space=pltpu.HBM)
+    dma = pltpu.SemaphoreType.DMA
+    return pl.pallas_call(
+        step_kernel,
+        name="step",
+        out_shape=(jax.ShapeDtypeStruct((own, embed), f32), jax.ShapeDtypeStruct((lines, 128), f32)),
+        in_specs=[vmem, hbm, hbm, hbm, hbm, vmem],
+        out_specs=(vmem, vmem),
+        scratch_shapes=[
+            pltpu.VMEM((users, features_in), bf16),
+            pltpu.VMEM((features_in, hidden), bf16),
+            pltpu.VMEM((hidden, embed), bf16),
+            pltpu.VMEM((width, embed), bf16),
+            pltpu.VMEM((users, embed), bf16),
+            pltpu.VMEM((users, embed), bf16),
+            pltpu.VMEM((NZ, NX - 1, per, width), f32),
+            pltpu.VMEM((NZ - 1, per, width), f32),
+            pltpu.VMEM((NZ - 1, per, width), f32),
+            pltpu.VMEM((16, own, embed), f32),
+            pltpu.VMEM((15, own, embed), f32),
+            pltpu.VMEM((own, embed), f32),
+            pltpu.VMEM((64, own, embed), f32),
+            pltpu.VMEM((2 * lines, 128), f32),
+            pltpu.VMEM((3, 2 * lines, 128), f32),
+            dma((4,)),
+            dma((NZ, NX - 1)),
+            dma((NZ, NX - 1)),
+            dma((NZ - 1,)),
+            dma((NZ - 1,)),
+            dma,
+            dma,
+            dma,
+            dma,
+            dma((3,)),
+            dma((3,)),
+        ],
+        compiler_params=pltpu.CompilerParams(collective_id=0, has_side_effects=True),
+        cost_estimate=pl.CostEstimate(flops=5 * 10**9, bytes_accessed=5 * 2**20, transcendentals=0),
+    )(partial, item_weight, features, user_w1, user_w2, places)
 
 
 def body(
     tables, bag_ids, bag_lengths, item_weight, user_features, user_w1, user_w2, positive_items
 ):
-    table = tables[0]
-    own_ids = bag_ids[0]
-    own_lengths = bag_lengths[0]
-    num_cand = lax.axis_size("cand")
-    num_dp = lax.axis_size("dp")
-    width = table.shape[1]
-    embed = item_weight.shape[1]
-    table_count = item_weight.shape[0] // width
-    partial = pool(own_ids.T, own_lengths[None, :], table)
-    per = partial.shape[0] // (NX * NZ)
-    partial = partial.reshape(NX, NZ, per, width).transpose(1, 0, 2, 3).reshape(partial.shape)
-    pooled = summed_on_arrival(partial, "tab", 0)
-    groups = num_cand * num_dp
-    shaped = pooled.reshape(1, groups, pooled.shape[0] // groups, width)
-    weight_blocks = item_weight.astype(jnp.float32).reshape(table_count, width, embed)
-    stacked = lax.all_to_all(shaped, ("cand", "dp"), split_axis=1, concat_axis=0, tiled=True)[:, 0]
-    item_pre = jnp.einsum(
-        "fbe,feh->bh",
-        stacked,
-        weight_blocks,
-        precision=lax.Precision.HIGHEST,
-        preferred_element_type=jnp.float32,
+    partial = pool(bag_ids[0].T, bag_lengths, tables[0])
+    item_emb, loss = step(
+        partial, item_weight, user_features, user_w1, user_w2, positive_items.reshape(-1, 128)
     )
-    item_emb = unit_rows(item_pre)
-    scale = logit_scale / embed
-    per_block = item_emb.shape[0]
-    cand_index = lax.axis_index("cand")
-
-    def make_adder(user_emb, positives):
-
-        def add_scores(carry, piece, global_id):
-            scores = (
-                lax.dot_general(
-                    user_emb,
-                    piece,
-                    (((1,), (1,)), ((), ())),
-                    precision=lax.Precision.HIGHEST,
-                    preferred_element_type=jnp.float32,
-                )
-                * scale
-            )
-            sums = jnp.sum(jnp.exp(scores), axis=1)
-            positive = jnp.sum(
-                jnp.where(global_id == positives[:, None], scores, jnp.float32(0.0)), axis=1
-            )
-            return (sums, positive)
-
-        return add_scores
-
-    user_emb = user_tower(user_features, user_w1, user_w2)
-    users_here = user_emb.shape[0]
-    start_carry = (jnp.zeros((users_here,), jnp.float32), jnp.zeros((users_here,), jnp.float32))
-    add_scores = make_adder(user_emb, positive_items)
-    piece = gather_directly(item_emb, ("tab", "dp"), 0)
-    place = lax.broadcasted_iota(jnp.int32, (1, piece.shape[0]), 1)
-    group = place // per_block
-    within = place % per_block
-    global_id = (
-        (group // num_dp * num_cand + cand_index) * num_dp + group % num_dp
-    ) * per_block + within
-    partial_sums = add_scores(start_carry, piece, global_id)
-    sums, positive = in_one((partial_sums[0], partial_sums[1]), "cand")
-    user_loss = jnp.log(sums) - positive
-    return (item_emb, user_loss)
+    return (item_emb, loss.reshape(-1))
 
 
 def solution(mesh):

time: 103 us -> 61.4 us (0.60)
  the two profiles are of different devices: /device:TPU:1 before, /device:TPU:7 now
where the time goes in v2:
time: 61.4 us; the launch traced here: 61.1 us
  Pallas kernels  57.9 us (94%)
  local copies, waits for them, and re-layouts  2.57 us (4%)
  between operations  0.65 us (1%)
    pallas_call x1, Pallas kernels, step(): pl.pallas_call(step_kernel, name='step', out_shape=(jax.ShapeDtypeStruct(...  47.4 us
    pallas_call x1, Pallas kernels, pool(): pl.pallas_call(pool_kernel, name='pool', out_shape=jax.ShapeDtypeStruct((...  10.5 us
    unnamed x2, local copies, waits for them, and re-layouts  2.57 us

profile of v2, /device:TPU:7, one launch (start us, length us, event | category | flops | bytes accessed | tf_op | source)
XLA Modules:
  0.0 61.1 jit_solution(537799114265492799)
XLA Ops:
  0.6 10.5 %pool.1.part_ref = f32[1024,128]{1,0:T(8,128)} custom-call(s32[16,1024]{1,0:T(8,128)} %bitcast.7, s32[1,1024]{1,0:T(1,128)} %len_ref.1, bf16[32768,128]{1,0:T(8,128)(2,1)} %bitcast.6), custom_call_target="tpu_custom_call" | custom-call | flops 100000000 | bytes 9437184 | tf_op jit(solution)/shard_map/pool/pallas_call | solution.py:134
  11.1 47.4 %step.1 = (f32[4,256]{1,0:T(4,128)}, f32[16,128]{1,0:T(8,128)}) custom-call(f32[1024,128]{1,0:T(8,128)} %pool.1.part_ref, bf16[2048,256]{1,0:T(8,128)(2,1)} %weight_ref.1, bf16[2048,512]{1,0:T(8,128)(2,1)} %x_ref.1, bf16[512,1024]{1,0:T(8,128)(2,1)} %w1_ref.1, bf16[1024,256]{1,0:T(8,128)(2,1)} %w2_ref.1, s32[16,128]{1,0:T(8,128)} %bitcast.9), custom_call_target="tpu_custom_call" | custom-call | flops 5000000000 | bytes 5242880 | tf_op jit(solution)/shard_map/step/pallas_call | solution.py:399
  58.6 1.3 %copy.12 = f32[4,256]{1,0:T(4,128)} copy(f32[4,256]{1,0:T(4,128)} %get-tuple-element.8) | data formatting | bytes 8192
  59.8 1.3 %copy.13 = f32[2048]{0:T(1024)} copy(f32[2048]{0:T(1024)} %bitcast.8) | data formatting | bytes 16384

commit v3 on v2

--- a/solution.py
+++ b/solution.py
@@ -14,29 +14,21 @@
 PARTS = 4
 DEPTH = 16
 CHUNKS = 8
+CAPACITY = 768
 
 
 def iota(shape, dim):
     return lax.broadcasted_iota(i32, shape, dim)
 
 
-def pool_kernel(ids_ref, len_ref, table_ref, out_ref, stage, tab, acc0, acc1, acc2, acc3,
+def list_kernel(ids_ref, len_ref, table_ref, list_out, extra_ref, stage, tab, acc0, acc1, acc2, acc3,
                 rank_ref, code_ref, list_ref, slist, load_sems, list_sem):
     rows = table_ref.shape[0]
     positions, items = ids_ref.shape
     tiles = items // 128
     chunk = rows // CHUNKS
     base = lax.axis_index("tab") * rows
-    loads = [
-        pltpu.make_async_copy(
-            table_ref.at[pl.ds(c * chunk, chunk)], stage.at[pl.ds(c * chunk, chunk)], load_sems.at[c]
-        )
-        for c in range(CHUNKS)
-    ]
-    for load in loads:
-        load.start()
     accs = (acc0, acc1, acc2, acc3)
-    dummy = items
 
     slots = tiles * positions
     ids = jnp.concatenate([ids_ref[:, 128 * t : 128 * (t + 1)] for t in range(tiles)], axis=0)
@@ -51,92 +43,126 @@
     per = items // (NX * NZ)
     block = lax.div(item, per)
     dest = (lax.rem(block, NX) * NZ + lax.div(block, NX)) * per + lax.rem(item, per)
-    code_ref[...] = local * 2048 + dest
-    livef = jnp.where(live, f32(1.0), f32(0.0)).astype(bf16)
+    code = local * 2048 + dest + 1
     below = jnp.where(iota((slots, slots), 0) >= iota((slots, slots), 1), f32(1.0), f32(0.0)).astype(bf16)
-    order = jnp.dot(below, livef, preferred_element_type=f32)
-    rank_ref[...] = jnp.where(live, order - 1.0, f32(-1.0)).astype(i32)
-    counts = order[slots - 1 : slots, :].astype(i32)
-    most = jnp.max(counts)
-
-    for acc in accs:
-        acc[...] = jnp.zeros_like(acc)
-
-    def convert(c):
-        loads[c].wait()
-
-        @pl.loop(0, chunk // 256)
+    ones = jnp.ones((128, 128), bf16)
+
+    def ordered(which):
+        marks = jnp.where(which, f32(1.0), f32(0.0)).astype(bf16)
+        order = jnp.dot(below, marks, preferred_element_type=f32)
+        return order, jnp.where(which, order - 1.0, f32(-1.0)).astype(i32)
+
+    order, rank = ordered(live)
+    counts = jnp.minimum(order[slots - 1 : slots, :], f32(DEPTH))
+    square = (128, 128)
+    before = iota(square, 0) < iota(square, 1)
+    offset = jnp.dot(
+        jnp.broadcast_to(counts, (8, 128)).astype(bf16),
+        jnp.where(before, f32(1.0), f32(0.0)).astype(bf16),
+        preferred_element_type=f32,
+    )
+    spread = jnp.broadcast_to(counts, square)
+    after = iota(square, 0) > iota(square, 1)
+    eye = iota(square, 0) == iota(square, 1)
+    column = jnp.dot(
+        jnp.concatenate([jnp.where(after, spread, f32(0.0)), jnp.where(eye, spread, f32(0.0))], axis=0).astype(bf16),
+        ones,
+        preferred_element_type=f32,
+    )
+    offset_column, count_column = column[:128].astype(i32), column[128:].astype(i32)
+    offset_row = offset[:1].astype(i32)
+    lane_square = iota(square, 1)
+    lines = iota((8, 128), 0)
+    left, right = [], []
+    for k in range(DEPTH):
+        found = jnp.sum(jnp.where(rank == k, code, 0), axis=0, keepdims=True)
+        where_to = jnp.broadcast_to(lax.shift_right_logical(offset_row + k, 7), (8, 128)) == lines
+        left.append(
+            jnp.concatenate(
+                [
+                    jnp.where(where_to, jnp.broadcast_to(lax.shift_right_logical(found, 7 * p) & 127, (8, 128)), 0)
+                    for p in range(4)
+                ],
+                axis=0,
+            ).astype(f32).astype(bf16)
+        )
+        hit = (((offset_column + k) & 127) == lane_square) & (count_column > k)
+        right.append(jnp.where(hit, f32(1.0), f32(0.0)).astype(bf16))
+    flat = jnp.dot(
+        jnp.concatenate(left, axis=1), jnp.concatenate(right, axis=0), preferred_element_type=f32
+    ).astype(i32)
+    list_out[...] = flat[:8] + flat[8:16] * 128 + flat[16:24] * 16384 + flat[24:32] * 2097152
+    extra_ref[...] = jnp.zeros_like(extra_ref)
+
+    place = offset_row + rank
+    over = live & ((rank >= DEPTH) | (place >= CAPACITY))
+    beyond = jnp.max(jnp.where(over, f32(1.0), f32(0.0)))
+
+    @pl.when(beyond > 0.0)
+    def _():
+        loads = [
+            pltpu.make_async_copy(
+                table_ref.at[pl.ds(c * chunk, chunk)], stage.at[pl.ds(c * chunk, chunk)], load_sems.at[c]
+            )
+            for c in range(CHUNKS)
+        ]
+        for load in loads:
+            load.start()
+        order, rank = ordered(over)
+        rank_ref[...] = rank
+        code_ref[...] = code
+        counts = order[slots - 1 : slots, :].astype(i32)
+        most = jnp.max(counts)
+        for acc in accs:
+            acc[...] = jnp.zeros_like(acc)
+        for load in loads:
+            load.wait()
+
+        @pl.loop(0, rows // 256)
         def _(s):
-            at = pl.ds(pl.multiple_of(c * chunk + s * 256, 256), 256)
+            at = pl.ds(pl.multiple_of(s * 256, 256), 256)
             tab[at, :] = stage[at, :].astype(f32)
 
-    def make_list(first):
-        for k in range(DEPTH):
-            found = jnp.sum(
-                jnp.where(rank_ref[...] == first + k, code_ref[...], 0), axis=0, keepdims=True
-            )
-            list_ref[k : k + 1, :] = jnp.where(counts > first + k, found, dummy)
-        list_ref[DEPTH : DEPTH + 1, :] = jnp.clip(counts - first, 0, DEPTH)
-
-    def add_listed():
-        @pl.loop(0, 128)
-        def _(at):
-            n = slist[DEPTH, at]
-
-            def group(g, _):
-                for q in range(PARTS):
-                    code = slist[g * PARTS + q, at]
-                    row = lax.shift_right_logical(code, 11)
-                    to = code & 2047
-                    accs[q][pl.ds(to, 1), :] += tab[pl.ds(row, 1), :]
-                return 0
-
-            lax.fori_loop(0, lax.shift_right_logical(n + PARTS - 1, 2), group, 0)
-
-    make_list(0)
-    copy = pltpu.make_async_copy(list_ref, slist, list_sem)
-    copy.start()
-    for c in range(CHUNKS):
-        convert(c)
-    copy.wait()
-    add_listed()
-
-    def more(b, _):
-        make_list(b * DEPTH)
-        copy = pltpu.make_async_copy(list_ref, slist, list_sem)
-        copy.start()
-        copy.wait()
-        add_listed()
-        return 0
-
-    lax.fori_loop(1, lax.div(most + DEPTH - 1, DEPTH), more, 0)
-
-    eye = iota((128, 128), 0) == iota((128, 128), 1)
-    ones = jnp.ones((128, 128), bf16)
-    for b in range(tiles):
-        parts = []
-        for h in range(128 // per):
-            to = b * (128 // per) + h
-            t = (to % NZ) * NX + to // NZ
-            parts.append(len_ref[:, t * per : (t + 1) * per])
-        row = jnp.concatenate(parts, axis=1).astype(f32)
-        spread = jnp.where(eye, jnp.broadcast_to(row, (128, 128)), f32(0.0)).astype(bf16)
-        column = jnp.dot(spread, ones, preferred_element_type=f32)
-        at = pl.ds(128 * b, 128)
-        out_ref[at, :] = (acc0[at, :] + acc1[at, :] + acc2[at, :] + acc3[at, :]) / column
-
-
-def pool(ids_t, lengths, table):
+        def more(b, _):
+            for k in range(DEPTH):
+                found = jnp.sum(
+                    jnp.where(rank_ref[...] == b * DEPTH + k, code_ref[...], 0), axis=0, keepdims=True
+                )
+                list_ref[k : k + 1, :] = found
+            list_ref[DEPTH : DEPTH + 1, :] = jnp.clip(counts - b * DEPTH, 0, DEPTH)
+            copy = pltpu.make_async_copy(list_ref, slist, list_sem)
+            copy.start()
+            copy.wait()
+
+            @pl.loop(0, 128)
+            def _(at):
+                def group(g, _):
+                    for q in range(PARTS):
+                        code = slist[g * PARTS + q, at]
+                        row = lax.shift_right_logical(code, 11)
+                        to = code & 2047
+                        accs[q][pl.ds(to, 1), :] += tab[pl.ds(row, 1), :]
+                    return 0
+
+                lax.fori_loop(0, lax.shift_right_logical(slist[DEPTH, at] + PARTS - 1, 2), group, 0)
+
+            return 0
+
+        lax.fori_loop(0, lax.div(most + DEPTH - 1, DEPTH), more, 0)
+        extra_ref[...] = acc0[1 : items + 1, :] + acc1[1 : items + 1, :] + acc2[1 : items + 1, :] + acc3[1 : items + 1, :]
+
+
+def make_list(ids_t, lengths, table):
     rows, width = table.shape
     positions, items = ids_t.shape
     slots = positions * items // 128
     vmem = pl.BlockSpec(memory_space=pltpu.VMEM)
     return pl.pallas_call(
-        pool_kernel,
-        name="pool",
-        out_shape=jax.ShapeDtypeStruct((items, width), f32),
+        list_kernel,
+        name="list",
+        out_shape=(jax.ShapeDtypeStruct((8, 128), i32), jax.ShapeDtypeStruct((items, width), f32)),
         in_specs=[vmem, vmem, pl.BlockSpec(memory_space=pltpu.HBM)],
-        out_specs=vmem,
+        out_specs=(vmem, vmem),
         scratch_shapes=[
             pltpu.VMEM((rows, width), bf16),
             pltpu.VMEM((rows, width), f32),
@@ -148,7 +174,8 @@
             pltpu.SemaphoreType.DMA((CHUNKS,)),
             pltpu.SemaphoreType.DMA,
         ],
-        cost_estimate=pl.CostEstimate(flops=10**8, bytes_accessed=9 * 2**20, transcendentals=0),
+        compiler_params=pltpu.CompilerParams(vmem_limit_bytes=58 * 2**20),
+        cost_estimate=pl.CostEstimate(flops=10**8, bytes_accessed=2**20, transcendentals=0),
     )(ids_t, lengths, table)
 
 
@@ -161,13 +188,14 @@
     return v * lax.rsqrt(jnp.mean(v * v, axis=-1, keepdims=True) + epsilon)
 
 
-PLAN = (1, 2, 1, 1, 3)
+PLAN = (0, 3, 1, 1, 3)
 USERS_AT_ONCE = 256
-
-
-def step_kernel(part_ref, weight_ref, x_ref, w1_ref, w2_ref, place_ref, item_ref, loss_ref,
-                xv, w1v, w2v, wv, high_ref, low_ref, recvx, sendz, recvz, sendt, recvt, embed_ref,
-                gathered, stats, others, load_sems, sx, rx, sz, rz, st, rt, sg, rg, ss, rs):
+TOGETHER = 16
+
+
+def step_kernel(slist, vlist, extra_ref, len_ref, table_ref, weight_ref, x_ref, w1_ref, w2_ref, place_ref, item_ref, loss_ref,
+                stage, wide, listed, part_ref, xv, w1v, w2v, wv, high_ref, low_ref, recvx, sendz, recvz, sendt, recvt, embed_ref,
+                gathered, stats, others, table_sems, load_sems, sx, rx, sz, rz, st, rt, sg, rg, ss, rs):
     tab, cand, dp = lax.axis_index("tab"), lax.axis_index("cand"), lax.axis_index("dp")
     xi, zi = lax.rem(tab, NX), lax.div(tab, NX)
     ntab, ncand, ndp = NX * NZ, 4, 4
@@ -181,6 +209,14 @@
         copy = pltpu.make_async_copy(src, dst, load_sems.at[k])
         copy.start()
         return copy
+
+    rows = table_ref.shape[0]
+    chunk = rows // CHUNKS
+    table_loads = []
+    for c in range(CHUNKS):
+        at = pl.ds(c * chunk, chunk)
+        table_loads.append(pltpu.make_async_copy(table_ref.at[at], stage.at[at], table_sems.at[c]))
+        table_loads[-1].start()
 
     loads = [
         local(x_ref, xv, 0),
@@ -224,7 +260,51 @@
             high_ref[at, :] = high
             low_ref[at, :] = low
 
-    tower(PLAN[0])
+    for c in range(CHUNKS):
+        table_loads[c].wait()
+
+        @pl.loop(0, chunk // 256)
+        def _(s):
+            at = pl.ds(pl.multiple_of(c * chunk + s * 256, 256), 256)
+            wide[at, :] = stage[at, :].astype(f32)
+
+    for line in range(CAPACITY // 128):
+
+        @pl.loop(0, 128 // TOGETHER)
+        def _(g):
+            at = pl.multiple_of(g * TOGETHER, TOGETHER)
+            fetched = []
+            for q in range(TOGETHER):
+                row = lax.shift_right_logical(slist[line, at + q], 11)
+                fetched.append(wide[pl.ds(row, 1), :])
+            for q in range(TOGETHER):
+                listed[pl.ds(line * 128 + at + q, 1), :] = fetched[q]
+
+    square = (128, 128)
+    eye = iota(square, 0) == iota(square, 1)
+    ones = jnp.ones(square, bf16)
+    picked = listed[...].astype(bf16)
+    wanted = vlist[...] & 2047
+    for b in range(part_ref.shape[0] // 128):
+        select = jnp.concatenate(
+            [
+                jnp.where(wanted[n : n + 1, :] == iota(square, 0) + (128 * b + 1), f32(1.0), f32(0.0)).astype(bf16)
+                for n in range(CAPACITY // 128)
+            ],
+            axis=1,
+        )
+        ends = []
+        for h in range(128 // per):
+            to = b * (128 // per) + h
+            t = (to % NZ) * NX + to // NZ
+            ends.append(len_ref[:, t * per : (t + 1) * per])
+        spread = jnp.broadcast_to(jnp.concatenate(ends, axis=1).astype(f32), square)
+        column = jnp.dot(jnp.where(eye, spread, f32(0.0)).astype(bf16), ones, preferred_element_type=f32)
+        at = pl.ds(128 * b, 128)
+        part_ref[at, :] = (jnp.dot(select, picked, preferred_element_type=f32) + extra_ref[at, :]) / column
+
+    if PLAN[0]:
+        tower(PLAN[0])
     pl.semaphore_wait(barrier, ntab * ndp - 1 + groups - ndp)
 
     xcopies = []
@@ -310,17 +390,20 @@
 
     me = tab * ndp + dp
 
-    @pl.loop(1, ntab * ndp)
-    def _(k):
-        peer = lax.rem(me + k, ntab * ndp)
-        pltpu.make_async_remote_copy(
-            src_ref=embed_ref,
-            dst_ref=gathered.at[me],
-            send_sem=sg,
-            recv_sem=rg,
-            device_id=(lax.div(peer, ndp), cand, lax.rem(peer, ndp)),
-            device_id_type=MESH,
-        ).start()
+    for k in turns:
+
+        @pl.loop(0 if k else 1, NX * ndp)
+        def _(n):
+            zp = lax.rem(zi + k, NZ)
+            xp = lax.rem(xi + lax.div(n, ndp), NX)
+            pltpu.make_async_remote_copy(
+                src_ref=embed_ref,
+                dst_ref=gathered.at[me],
+                send_sem=sg,
+                recv_sem=rg,
+                device_id=(zp * NX + xp, cand, lax.rem(dp + n, ndp)),
+                device_id_type=MESH,
+            ).start()
 
     gathered[me] = embed
     tower(PLAN[4])
@@ -356,7 +439,7 @@
             stats[pl.ds(line + place_ref.shape[0], 1), :] = positive
         return 0
 
-    lax.fori_loop(0, xv.shape[0] // USERS_AT_ONCE, score, 0)
+    lax.fori_loop(0, xv.shape[0] // USERS_AT_ONCE, score, 0, unroll=4)
 
     scopies = []
     for o in range(1, ncand):
@@ -386,8 +469,9 @@
         copy.wait_send()
 
 
-def step(partial, item_weight, features, user_w1, user_w2, places):
-    items, width = partial.shape
+def step(flat, extra, lengths, table, item_weight, features, user_w1, user_w2, places):
+    items, width = extra.shape
+    rows = table.shape[0]
     users, features_in = features.shape
     hidden, embed = user_w2.shape
     per = items // (NX * NZ)
@@ -400,9 +484,13 @@
         step_kernel,
         name="step",
         out_shape=(jax.ShapeDtypeStruct((own, embed), f32), jax.ShapeDtypeStruct((lines, 128), f32)),
-        in_specs=[vmem, hbm, hbm, hbm, hbm, vmem],
+        in_specs=[pl.BlockSpec(memory_space=pltpu.SMEM), vmem, vmem, vmem, hbm, hbm, hbm, hbm, hbm, vmem],
         out_specs=(vmem, vmem),
         scratch_shapes=[
+            pltpu.VMEM((rows, width), bf16),
+            pltpu.VMEM((rows, width), f32),
+            pltpu.VMEM((CAPACITY, width), f32),
+            pltpu.VMEM((items, width), f32),
             pltpu.VMEM((users, features_in), bf16),
             pltpu.VMEM((features_in, hidden), bf16),
             pltpu.VMEM((hidden, embed), bf16),
@@ -418,6 +506,7 @@
             pltpu.VMEM((64, own, embed), f32),
             pltpu.VMEM((2 * lines, 128), f32),
             pltpu.VMEM((3, 2 * lines, 128), f32),
+            dma((CHUNKS,)),
             dma((4,)),
             dma((NZ, NX - 1)),
             dma((NZ, NX - 1)),
@@ -430,17 +519,19 @@
             dma((3,)),
             dma((3,)),
         ],
-        compiler_params=pltpu.CompilerParams(collective_id=0, has_side_effects=True),
+        compiler_params=pltpu.CompilerParams(
+            collective_id=0, has_side_effects=True, vmem_limit_bytes=48 * 2**20
+        ),
         cost_estimate=pl.CostEstimate(flops=5 * 10**9, bytes_accessed=5 * 2**20, transcendentals=0),
-    )(partial, item_weight, features, user_w1, user_w2, places)
+    )(flat, flat, extra, lengths, table, item_weight, features, user_w1, user_w2, places)
 
 
 def body(
     tables, bag_ids, bag_lengths, item_weight, user_features, user_w1, user_w2, positive_items
 ):
-    partial = pool(bag_ids[0].T, bag_lengths, tables[0])
+    flat, extra = make_list(bag_ids[0].T, bag_lengths, tables[0])
     item_emb, loss = step(
-        partial, item_weight, user_features, user_w1, user_w2, positive_items.reshape(-1, 128)
+        flat, extra, bag_lengths, tables[0], item_weight, user_features, user_w1, user_w2, positive_items.reshape(-1, 128)
     )
     return (item_emb, loss.reshape(-1))
 

time: 61.4 us -> 53 us (0.86)
  the two profiles are of different devices: /device:TPU:7 before, /device:TPU:1 now
where the time goes in v3:
time: 53 us; the launch traced here: 52.4 us
  Pallas kernels  48.7 us (92%)
  local copies, waits for them, and re-layouts  2.94 us (6%)
  between operations  0.75 us (1%)
    pallas_call x1, Pallas kernels, step(): pl.pallas_call(step_kernel, name='step', out_shape=(jax.ShapeDtypeStruct(...  46 us
    unnamed x18, local copies, waits for them, and re-layouts  2.94 us
    pallas_call x1, Pallas kernels, make_list(): pl.pallas_call(list_kernel, name='list', out_shape=(jax.ShapeDtypeStruct(...  2.64 us

profile of v3, /device:TPU:1, one launch (start us, length us, event | category | flops | bytes accessed | tf_op | source)
XLA Modules:
  0.0 52.4 jit_solution(15944973020713806926)
XLA Ops:
  0.6 0.0 copy-start
  0.6 0.0 copy-start.6
  0.7 0.0 copy-start.4
  0.7 0.0 copy-start.3
  0.7 0.0 copy-start.1
  0.7 0.0 copy-start.2
  0.7 2.6 %list.1 = (s32[8,128]{1,0:T(8,128)}, f32[1024,128]{1,0:T(8,128)}) custom-call(s32[16,1024]{1,0:T(8,128)} %bitcast.10, s32[1,1024]{1,0:T(1,128)} %len_ref.3, bf16[32768,128]{1,0:T(8,128)(2,1)} %bitcast.8), custom_call_target="tpu_custom_call" | custom-call | flops 100000000 | bytes 1048576 | tf_op jit(solution)/shard_map/list/pallas_call | solution.py:160
  3.3 0.0 copy-done
  3.4 0.0 copy-done.6
  3.4 0.0 copy-done.4
  3.4 0.0 copy-done.3
  3.4 0.0 copy-done.1
  3.4 0.0 copy-done.2
  3.4 0.0 copy-start.5
  3.4 1.0 %copy-done.5 = f32[1024,128]{1,0:T(8,128)S(1)} copy-done((f32[1024,128]{1,0:T(8,128)S(1)}, f32[1024,128]{1,0:T(8,128)}, u32[]{:S(2)}) %copy-start.5) | copy-done | bytes 524312
  4.4 0.0 copy-start.7
  4.4 0.7 %copy-done.7 = s32[8,128]{1,0:T(8,128)S(1)} copy-done((s32[8,128]{1,0:T(8,128)S(1)}, s32[8,128]{1,0:T(8,128)}, u32[]{:S(2)}) %copy-start.7) | copy-done | bytes 4120
  5.1 46.0 %step.1 = (f32[4,256]{1,0:T(4,128)S(1)}, f32[16,128]{1,0:T(8,128)S(1)}) custom-call(s32[8,128]{1,0:T(8,128)S(1)} %copy-done.7, s32[8,128]{1,0:T(8,128)S(1)} %copy-done.7, f32[1024,128]{1,0:T(8,128)S(1)} %copy-done.5, s32[1,1024]{1,0:T(1,128)S(1)} %copy-done, bf16[32768,128]{1,0:T(8,128)(2,1)} %bitcast.9, bf16[2048,256]{1,0:T(8,128)(2,1)S(1)} %copy-done.2, ...), custom_call_target="tpu_custom_call" | custom-call | flops 5000000000 | bytes 5242880 | tf_op jit(solution)/shard_map/step/pallas_call | solution.py:483
  51.2 0.6 %copy.12 = f32[4,256]{1,0:T(4,128)} copy(f32[4,256]{1,0:T(4,128)S(1)} %get-tuple-element.12) | data formatting | bytes 8192
  51.8 0.6 %copy.13 = f32[2048]{0:T(1024)} copy(f32[2048]{0:T(1024)S(1)} %bitcast.6) | data formatting | bytes 16384
Async XLA Ops:
  0.6 2.7 %copy-start = (s32[1,1024]{1,0:T(1,128)S(1)}, s32[1,1024]{1,0:T(1,128)}, u32[]{:S(2)}) copy-start(s32[1,1024]{1,0:T(1,128)} %len_ref.3) | copy-start | bytes 12292
  0.6 2.7 %copy-start.6 = (s32[2048]{0:T(1024)S(1)}, s32[2048]{0:T(1024)}, u32[]{:S(2)}) copy-start(s32[2048]{0:T(1024)} %param.15) | copy-start | bytes 24580
  0.7 2.7 %copy-start.4 = (bf16[1024,256]{1,0:T(8,128)(2,1)S(1)}, bf16[1024,256]{1,0:T(8,128)(2,1)}, u32[]{:S(2)}) copy-start(bf16[1024,256]{1,0:T(8,128)(2,1)} %w2_ref.1) | copy-start | bytes 1572868
  0.7 2.7 %copy-start.3 = (bf16[512,1024]{1,0:T(8,128)(2,1)S(1)}, bf16[512,1024]{1,0:T(8,128)(2,1)}, u32[]{:S(2)}) copy-start(bf16[512,1024]{1,0:T(8,128)(2,1)} %w1_ref.1) | copy-start | bytes 3145732
  0.7 2.7 %copy-start.1 = (bf16[2048,512]{1,0:T(8,128)(2,1)S(1)}, bf16[2048,512]{1,0:T(8,128)(2,1)}, u32[]{:S(2)}) copy-start(bf16[2048,512]{1,0:T(8,128)(2,1)} %x_ref.1) | copy-start | bytes 6291460
  0.7 2.7 %copy-start.2 = (bf16[2048,256]{1,0:T(8,128)(2,1)S(1)}, bf16[2048,256]{1,0:T(8,128)(2,1)}, u32[]{:S(2)}) copy-start(bf16[2048,256]{1,0:T(8,128)(2,1)} %weight_ref.1) | copy-start | bytes 3145732
  3.4 1.0 %copy-start.5 = (f32[1024,128]{1,0:T(8,128)S(1)}, f32[1024,128]{1,0:T(8,128)}, u32[]{:S(2)}) copy-start(f32[1024,128]{1,0:T(8,128)} %get-tuple-element.7.extra_ref) | copy-start | bytes 1572868
  4.4 0.7 %copy-start.7 = (s32[8,128]{1,0:T(8,128)S(1)}, s32[8,128]{1,0:T(8,128)}, u32[]{:S(2)}) copy-start(s32[8,128]{1,0:T(8,128)} %get-tuple-element.6.slist.vlist) | copy-start | bytes 12292

commit v4 on v3

--- a/solution.py
+++ b/solution.py
@@ -174,7 +174,7 @@
             pltpu.SemaphoreType.DMA((CHUNKS,)),
             pltpu.SemaphoreType.DMA,
         ],
-        compiler_params=pltpu.CompilerParams(vmem_limit_bytes=58 * 2**20),
+        compiler_params=pltpu.CompilerParams(vmem_limit_bytes=52 * 2**20),
         cost_estimate=pl.CostEstimate(flops=10**8, bytes_accessed=2**20, transcendentals=0),
     )(ids_t, lengths, table)
 
@@ -193,9 +193,9 @@
 TOGETHER = 16
 
 
-def step_kernel(slist, vlist, extra_ref, len_ref, table_ref, weight_ref, x_ref, w1_ref, w2_ref, place_ref, item_ref, loss_ref,
-                stage, wide, listed, part_ref, xv, w1v, w2v, wv, high_ref, low_ref, recvx, sendz, recvz, sendt, recvt, embed_ref,
-                gathered, stats, others, table_sems, load_sems, sx, rx, sz, rz, st, rt, sg, rg, ss, rs):
+def step_kernel(slist, vlist, extra_ref, len_ref, table_ref, weight_ref, xv, w1v, w2v, place_ref, item_ref, loss_ref,
+                stage, wide, listed, part_ref, high_ref, low_ref, recvx, sendz, recvz, sendt, recvt, embed_ref,
+                gathered, stats, others, table_sems, sx, rx, sz, rz, st, rt, sg, rg, ss, rs):
     tab, cand, dp = lax.axis_index("tab"), lax.axis_index("cand"), lax.axis_index("dp")
     xi, zi = lax.rem(tab, NX), lax.div(tab, NX)
     ntab, ncand, ndp = NX * NZ, 4, 4
@@ -205,11 +205,6 @@
     own = per // groups
     table = cand * ndp + dp
 
-    def local(src, dst, k):
-        copy = pltpu.make_async_copy(src, dst, load_sems.at[k])
-        copy.start()
-        return copy
-
     rows = table_ref.shape[0]
     chunk = rows // CHUNKS
     table_loads = []
@@ -218,35 +213,23 @@
         table_loads.append(pltpu.make_async_copy(table_ref.at[at], stage.at[at], table_sems.at[c]))
         table_loads[-1].start()
 
-    loads = [
-        local(x_ref, xv, 0),
-        local(w1_ref, w1v, 1),
-        local(w2_ref, w2v, 2),
-        local(weight_ref.at[pl.ds(pl.multiple_of(table * width, width), width)], wv, 3),
-    ]
-
     barrier = pltpu.get_barrier_semaphore()
 
-    @pl.loop(1, ntab * ndp)
-    def _(k):
-        peer = lax.rem(tab * ndp + dp + k, ntab * ndp)
-        pl.semaphore_signal(
-            barrier, inc=1, device_id=(lax.div(peer, ndp), cand, lax.rem(peer, ndp)), device_id_type=MESH
-        )
-
-    @pl.loop(ndp, groups)
-    def _(k):
-        peer = lax.rem(cand * ndp + k, groups)
-        pl.semaphore_signal(
-            barrier, inc=1, device_id=(tab, lax.div(peer, ndp), lax.rem(peer, ndp)), device_id_type=MESH
-        )
+    def greet(device):
+        pl.semaphore_signal(barrier, inc=1, device_id=device, device_id_type=MESH)
+
+    for a in (2, 3, 1, 0):
+        for k in (2, 1, 3, 0):
+            if a or k:
+                greet((tab, lax.rem(cand + a, ncand), lax.rem(dp + k, ndp)))
+    for k in range(1, NZ):
+        greet((lax.rem(zi + k, NZ) * NX + xi, cand, dp))
+    for k in range(1, NX):
+        greet((zi * NX + lax.rem(xi + k, NX), cand, dp))
 
     done = [0]
 
     def tower(chunks):
-        if done[0] == 0:
-            for k in range(3):
-                loads[k].wait()
         first = done[0]
         done[0] += chunks
 
@@ -305,7 +288,7 @@
 
     if PLAN[0]:
         tower(PLAN[0])
-    pl.semaphore_wait(barrier, ntab * ndp - 1 + groups - ndp)
+    pl.semaphore_wait(barrier, groups - 1 + NZ - 1 + NX - 1)
 
     xcopies = []
     turns = (2, 1, 3, 0)
@@ -352,31 +335,32 @@
             copy.start()
             zcopies.append(copy)
     tower(PLAN[2])
-    loads[3].wait()
     for copy in zcopies:
         copy.wait_recv()
     pooled = pooled + recvz[0] + recvz[1] + recvz[2]
 
+    mine_at = pl.ds(pl.multiple_of(table * width, width), width)
     p0 = pooled.astype(bf16)
     rest = pooled - p0.astype(f32)
     p1 = rest.astype(bf16)
     p2 = (rest - p1.astype(f32)).astype(bf16)
-    terms = jnp.dot(jnp.concatenate([p0, p1, p2], axis=0), wv[...], preferred_element_type=f32)
+    terms = jnp.dot(jnp.concatenate([p0, p1, p2], axis=0), weight_ref[mine_at, :], preferred_element_type=f32)
     terms = terms[:per] + terms[per : 2 * per] + terms[2 * per :]
     for b in range(groups):
         sendt[b] = terms[b * own : (b + 1) * own, :]
 
-    @pl.loop(1, groups)
-    def _(k):
-        peer = lax.rem(table + k, groups)
-        pltpu.make_async_remote_copy(
-            src_ref=sendt.at[peer],
-            dst_ref=recvt.at[k - 1],
-            send_sem=st,
-            recv_sem=rt,
-            device_id=(tab, lax.div(peer, ndp), lax.rem(peer, ndp)),
-            device_id_type=MESH,
-        ).start()
+    for a in (2, 3, 1, 0):
+        for k in (2, 1, 3, 0):
+            if a or k:
+                there, that = lax.rem(cand + a, ncand), lax.rem(dp + k, ndp)
+                pltpu.make_async_remote_copy(
+                    src_ref=sendt.at[there * ndp + that],
+                    dst_ref=recvt.at[a * ndp + k - 1],
+                    send_sem=st,
+                    recv_sem=rt,
+                    device_id=(tab, there, that),
+                    device_id_type=MESH,
+                ).start()
 
     tower(PLAN[3])
     all_t = pltpu.make_async_copy(recvt, recvt, rt)
@@ -472,8 +456,7 @@
 def step(flat, extra, lengths, table, item_weight, features, user_w1, user_w2, places):
     items, width = extra.shape
     rows = table.shape[0]
-    users, features_in = features.shape
-    hidden, embed = user_w2.shape
+    users, embed = features.shape[0], user_w2.shape[1]
     per = items // (NX * NZ)
     own = per // 16
     lines = users // 128
@@ -484,17 +467,13 @@
         step_kernel,
         name="step",
         out_shape=(jax.ShapeDtypeStruct((own, embed), f32), jax.ShapeDtypeStruct((lines, 128), f32)),
-        in_specs=[pl.BlockSpec(memory_space=pltpu.SMEM), vmem, vmem, vmem, hbm, hbm, hbm, hbm, hbm, vmem],
+        in_specs=[pl.BlockSpec(memory_space=pltpu.SMEM), vmem, vmem, vmem, hbm, *[vmem] * 5],
         out_specs=(vmem, vmem),
         scratch_shapes=[
             pltpu.VMEM((rows, width), bf16),
             pltpu.VMEM((rows, width), f32),
             pltpu.VMEM((CAPACITY, width), f32),
             pltpu.VMEM((items, width), f32),
-            pltpu.VMEM((users, features_in), bf16),
-            pltpu.VMEM((features_in, hidden), bf16),
-            pltpu.VMEM((hidden, embed), bf16),
-            pltpu.VMEM((width, embed), bf16),
             pltpu.VMEM((users, embed), bf16),
             pltpu.VMEM((users, embed), bf16),
             pltpu.VMEM((NZ, NX - 1, per, width), f32),
@@ -507,7 +486,6 @@
             pltpu.VMEM((2 * lines, 128), f32),
             pltpu.VMEM((3, 2 * lines, 128), f32),
             dma((CHUNKS,)),
-            dma((4,)),
             dma((NZ, NX - 1)),
             dma((NZ, NX - 1)),
             dma((NZ - 1,)),
@@ -520,7 +498,7 @@
             dma((3,)),
         ],
         compiler_params=pltpu.CompilerParams(
-            collective_id=0, has_side_effects=True, vmem_limit_bytes=48 * 2**20
+            collective_id=0, has_side_effects=True, vmem_limit_bytes=46 * 2**20
         ),
         cost_estimate=pl.CostEstimate(flops=5 * 10**9, bytes_accessed=5 * 2**20, transcendentals=0),
     )(flat, flat, extra, lengths, table, item_weight, features, user_w1, user_w2, places)

time: 53 us -> 50.3 us (0.949)
  Pallas kernels: 48.7 us -> 45.3 us
  local copies, waits for them, and re-layouts: 2.94 us -> 4.17 us
    pallas_call x1, Pallas kernels: 2.64 us -> 0.83 us  [make_list(): pl.pallas_call(list_kernel, name='list', out_shape=(jax.ShapeDtypeStruct(...]
    pallas_call x1, Pallas kernels: 46 us -> 44.5 us  [step(): pl.pallas_call(step_kernel, name='step', out_shape=(jax.ShapeDtypeStruct(...]
    unnamed x18 -> x16, local copies, waits for them, and re-layouts: 2.94 us -> 4.17 us
where the time goes in v4:
time: 50.3 us; the launch traced here: 50.1 us
  Pallas kernels  45.3 us (90%)
  local copies, waits for them, and re-layouts  4.17 us (8%)
  between operations  0.67 us (1%)
    pallas_call x1, Pallas kernels, step(): pl.pallas_call(step_kernel, name='step', out_shape=(jax.ShapeDtypeStruct(...  44.5 us
    unnamed x16, local copies, waits for them, and re-layouts  4.17 us

profile of v4, /device:TPU:1, one launch (start us, length us, event | category | flops | bytes accessed | tf_op | source)
XLA Modules:
  0.0 50.1 jit_solution(17638590012747398064)
XLA Ops:
  0.6 0.0 copy-start
  0.6 0.8 %copy-done = s32[1,1024,16]{1,2,0:T(8,128)S(1)} copy-done((s32[1,1024,16]{1,2,0:T(8,128)S(1)}, s32[1,1024,16]{1,2,0:T(8,128)}, u32[]{:S(2)}) %copy-start) | copy-done | bytes 65560
  1.5 0.0 copy-start.1
  1.5 0.7 %copy-done.1 = s32[1,1024]{1,0:T(1,128)S(1)} copy-done((s32[1,1024]{1,0:T(1,128)S(1)}, s32[1,1024]{1,0:T(1,128)}, u32[]{:S(2)}) %copy-start.1) | copy-done | bytes 4120
  2.2 0.0 copy-start.2
  2.2 0.0 copy-start.3
  2.2 0.0 copy-start.4
  2.2 0.0 copy-start.5
  2.2 0.0 copy-start.6
  2.2 0.8 %list.1 = (s32[8,128]{1,0:T(8,128)S(1)}, f32[1024,128]{1,0:T(8,128)S(1)}) custom-call(s32[16,1024]{1,0:T(8,128)S(1)} %bitcast.6, s32[1,1024]{1,0:T(1,128)S(1)} %copy-done.1, bf16[32768,128]{1,0:T(8,128)(2,1)} %bitcast.9), custom_call_target="tpu_custom_call" | custom-call | flops 100000000 | bytes 1048576 | tf_op jit(solution)/shard_map/list/pallas_call | solution.py:160
  3.0 0.7 %copy-done.2 = bf16[2048,512]{1,0:T(8,128)(2,1)S(1)} copy-done((bf16[2048,512]{1,0:T(8,128)(2,1)S(1)}, bf16[2048,512]{1,0:T(8,128)(2,1)}, u32[]{:S(2)}) %copy-start.2) | copy-done | bytes 2097176
  3.8 0.3 copy-done.3
  4.0 0.3 copy-done.4
  4.3 0.1 copy-done.5
  4.5 0.0 copy-done.6
  4.5 44.5 %step.1 = (f32[4,256]{1,0:T(4,128)S(1)}, f32[16,128]{1,0:T(8,128)S(1)}) custom-call(s32[8,128]{1,0:T(8,128)S(1)} %get-tuple-element.6.slist.vlist, s32[8,128]{1,0:T(8,128)S(1)} %get-tuple-element.6.slist.vlist, f32[1024,128]{1,0:T(8,128)S(1)} %get-tuple-element.7.extra_ref, s32[1,1024]{1,0:T(1,128)S(1)} %copy-done.1, bf16[32768,128]{1,0:T(8,128)(2,1)} %bitcast.10, ...), custom_call_target="tpu_custom_call" | custom-call | flops 5000000000 | bytes 5242880 | tf_op jit(solution)/shard_map/step/pallas_call | solution.py:466
  48.9 0.6 %copy.12 = f32[4,256]{1,0:T(4,128)} copy(f32[4,256]{1,0:T(4,128)S(1)} %get-tuple-element.12) | data formatting | bytes 8192
  49.5 0.6 %copy.13 = f32[2048]{0:T(1024)} copy(f32[2048]{0:T(1024)S(1)} %bitcast.7) | data formatting | bytes 16384
Async XLA Ops:
  0.6 0.8 %copy-start = (s32[1,1024,16]{1,2,0:T(8,128)S(1)}, s32[1,1024,16]{1,2,0:T(8,128)}, u32[]{:S(2)}) copy-start(s32[1,1024,16]{1,2,0:T(8,128)} %param.9) | copy-start | bytes 196612
  1.5 0.7 %copy-start.1 = (s32[1,1024]{1,0:T(1,128)S(1)}, s32[1,1024]{1,0:T(1,128)}, u32[]{:S(2)}) copy-start(s32[1,1024]{1,0:T(1,128)} %len_ref.3) | copy-start | bytes 12292
  2.2 1.6 %copy-start.2 = (bf16[2048,512]{1,0:T(8,128)(2,1)S(1)}, bf16[2048,512]{1,0:T(8,128)(2,1)}, u32[]{:S(2)}) copy-start(bf16[2048,512]{1,0:T(8,128)(2,1)} %xv.1) | copy-start | bytes 6291460
  2.2 1.9 %copy-start.3 = (bf16[2048,256]{1,0:T(8,128)(2,1)S(1)}, bf16[2048,256]{1,0:T(8,128)(2,1)}, u32[]{:S(2)}) copy-start(bf16[2048,256]{1,0:T(8,128)(2,1)} %weight_ref.1) | copy-start | bytes 3145732
  2.2 2.2 %copy-start.4 = (bf16[512,1024]{1,0:T(8,128)(2,1)S(1)}, bf16[512,1024]{1,0:T(8,128)(2,1)}, u32[]{:S(2)}) copy-start(bf16[512,1024]{1,0:T(8,128)(2,1)} %w1v.1) | copy-start | bytes 3145732
  2.2 2.3 %copy-start.5 = (bf16[1024,256]{1,0:T(8,128)(2,1)S(1)}, bf16[1024,256]{1,0:T(8,128)(2,1)}, u32[]{:S(2)}) copy-start(bf16[1024,256]{1,0:T(8,128)(2,1)} %w2v.1) | copy-start | bytes 1572868
  2.2 2.3 %copy-start.6 = (s32[2048]{0:T(1024)S(1)}, s32[2048]{0:T(1024)}, u32[]{:S(2)}) copy-start(s32[2048]{0:T(1024)} %param.15) | copy-start | bytes 24580

commit v5 on v4

--- a/solution.py
+++ b/solution.py
@@ -14,14 +14,16 @@
 PARTS = 4
 DEPTH = 16
 CHUNKS = 8
-CAPACITY = 768
+CAPACITY = 704
+LINES = 6
+LANE_DEPTH = 20
 
 
 def iota(shape, dim):
     return lax.broadcasted_iota(i32, shape, dim)
 
 
-def list_kernel(ids_ref, len_ref, table_ref, list_out, extra_ref, stage, tab, acc0, acc1, acc2, acc3,
+def list_kernel(ids_ref, table_ref, list_out, extra_ref, stage, tab, acc0, acc1, acc2, acc3,
                 rank_ref, code_ref, list_ref, slist, load_sems, list_sem):
     rows = table_ref.shape[0]
     positions, items = ids_ref.shape
@@ -32,13 +34,10 @@
 
     slots = tiles * positions
     ids = jnp.concatenate([ids_ref[:, 128 * t : 128 * (t + 1)] for t in range(tiles)], axis=0)
-    lengths = jnp.concatenate(
-        [jnp.broadcast_to(len_ref[:, 128 * t : 128 * (t + 1)], (positions, 128)) for t in range(tiles)], axis=0
-    )
     r = iota((slots, 128), 0)
     lane = iota((slots, 128), 1)
     local = ids - base
-    live = (local >= 0) & (local < rows) & (lax.rem(r, positions) < lengths)
+    live = (local >= 0) & (local < rows)
     item = lax.div(r, positions) * 128 + lane
     per = items // (NX * NZ)
     block = lax.div(item, per)
@@ -53,7 +52,7 @@
         return order, jnp.where(which, order - 1.0, f32(-1.0)).astype(i32)
 
     order, rank = ordered(live)
-    counts = jnp.minimum(order[slots - 1 : slots, :], f32(DEPTH))
+    counts = jnp.minimum(order[slots - 1 : slots, :], f32(LANE_DEPTH))
     square = (128, 128)
     before = iota(square, 0) < iota(square, 1)
     offset = jnp.dot(
@@ -74,7 +73,7 @@
     lane_square = iota(square, 1)
     lines = iota((8, 128), 0)
     left, right = [], []
-    for k in range(DEPTH):
+    for k in range(LANE_DEPTH):
         found = jnp.sum(jnp.where(rank == k, code, 0), axis=0, keepdims=True)
         where_to = jnp.broadcast_to(lax.shift_right_logical(offset_row + k, 7), (8, 128)) == lines
         left.append(
@@ -91,11 +90,13 @@
     flat = jnp.dot(
         jnp.concatenate(left, axis=1), jnp.concatenate(right, axis=0), preferred_element_type=f32
     ).astype(i32)
-    list_out[...] = flat[:8] + flat[8:16] * 128 + flat[16:24] * 16384 + flat[24:32] * 2097152
+    codes = flat[:8] + flat[8:16] * 128 + flat[16:24] * 16384 + flat[24:32] * 2097152
+    list_out[:8, :] = lax.shift_right_logical(codes, 11)
+    list_out[8:, :] = codes & 2047
     extra_ref[...] = jnp.zeros_like(extra_ref)
 
     place = offset_row + rank
-    over = live & ((rank >= DEPTH) | (place >= CAPACITY))
+    over = live & ((rank >= LANE_DEPTH) | (place >= CAPACITY))
     beyond = jnp.max(jnp.where(over, f32(1.0), f32(0.0)))
 
     @pl.when(beyond > 0.0)
@@ -152,7 +153,7 @@
         extra_ref[...] = acc0[1 : items + 1, :] + acc1[1 : items + 1, :] + acc2[1 : items + 1, :] + acc3[1 : items + 1, :]
 
 
-def make_list(ids_t, lengths, table):
+def make_list(ids_t, table):
     rows, width = table.shape
     positions, items = ids_t.shape
     slots = positions * items // 128
@@ -160,8 +161,8 @@
     return pl.pallas_call(
         list_kernel,
         name="list",
-        out_shape=(jax.ShapeDtypeStruct((8, 128), i32), jax.ShapeDtypeStruct((items, width), f32)),
-        in_specs=[vmem, vmem, pl.BlockSpec(memory_space=pltpu.HBM)],
+        out_shape=(jax.ShapeDtypeStruct((16, 128), i32), jax.ShapeDtypeStruct((items, width), f32)),
+        in_specs=[vmem, pl.BlockSpec(memory_space=pltpu.HBM)],
         out_specs=(vmem, vmem),
         scratch_shapes=[
             pltpu.VMEM((rows, width), bf16),
@@ -176,7 +177,7 @@
         ],
         compiler_params=pltpu.CompilerParams(vmem_limit_bytes=52 * 2**20),
         cost_estimate=pl.CostEstimate(flops=10**8, bytes_accessed=2**20, transcendentals=0),
-    )(ids_t, lengths, table)
+    )(ids_t, table)
 
 
 def split2(v):
@@ -191,11 +192,12 @@
 PLAN = (0, 3, 1, 1, 3)
 USERS_AT_ONCE = 256
 TOGETHER = 16
-
-
-def step_kernel(slist, vlist, extra_ref, len_ref, table_ref, weight_ref, xv, w1v, w2v, place_ref, item_ref, loss_ref,
-                stage, wide, listed, part_ref, high_ref, low_ref, recvx, sendz, recvz, sendt, recvt, embed_ref,
-                gathered, stats, others, table_sems, sx, rx, sz, rz, st, rt, sg, rg, ss, rs):
+UNROLL = 4
+
+
+def step_kernel(vlist, extra_ref, len_ref, table_ref, weight_ref, x_ref, w1_ref, w2_ref, place_ref, item_ref, loss_ref,
+                stage, wide, listed, part_ref, xv, w1v, w2v, wv, high_ref, low_ref, recvx, sendz, recvz, sendt, recvt, embed_ref,
+                gathered, stats, others, slist, list_sem, table_sems, load_sems, sx, rx, sz, rz, st, rt, sg, rg, ss, rs):
     tab, cand, dp = lax.axis_index("tab"), lax.axis_index("cand"), lax.axis_index("dp")
     xi, zi = lax.rem(tab, NX), lax.div(tab, NX)
     ntab, ncand, ndp = NX * NZ, 4, 4
@@ -205,6 +207,12 @@
     own = per // groups
     table = cand * ndp + dp
 
+    list_copy = pltpu.make_async_copy(vlist.at[pl.ds(0, 8)], slist, list_sem)
+    list_copy.start()
+
+    def local(src, dst, k):
+        return pltpu.make_async_copy(src, dst, load_sems.at[k])
+
     rows = table_ref.shape[0]
     chunk = rows // CHUNKS
     table_loads = []
@@ -212,6 +220,13 @@
         at = pl.ds(c * chunk, chunk)
         table_loads.append(pltpu.make_async_copy(table_ref.at[at], stage.at[at], table_sems.at[c]))
         table_loads[-1].start()
+
+    loads = [
+        local(x_ref, xv, 0),
+        local(w1_ref, w1v, 1),
+        local(w2_ref, w2v, 2),
+        local(weight_ref.at[pl.ds(pl.multiple_of(table * width, width), width)], wv, 3),
+    ]
 
     barrier = pltpu.get_barrier_semaphore()
 
@@ -230,6 +245,9 @@
     done = [0]
 
     def tower(chunks):
+        if done[0] == 0:
+            for k in range(3):
+                loads[k].wait()
         first = done[0]
         done[0] += chunks
 
@@ -239,27 +257,31 @@
             hidden = jnp.dot(xv[at, :], w1v[...], preferred_element_type=f32)
             hidden = (0.5 * hidden * (1.0 + lax.erf(hidden * f32(0.5**0.5)))).astype(bf16)
             users = unit_rows(jnp.dot(hidden, w2v[...], preferred_element_type=f32))
-            high, low = split2(users * (logit_scale / users.shape[1]))
-            high_ref[at, :] = high
-            low_ref[at, :] = low
+            high, low = split2((users * (logit_scale / users.shape[1])).T)
+            high_ref[:, at] = high
+            low_ref[:, at] = low
 
     for c in range(CHUNKS):
         table_loads[c].wait()
+        if c == CHUNKS - 2:
+            for load in loads:
+                load.start()
 
         @pl.loop(0, chunk // 256)
         def _(s):
             at = pl.ds(pl.multiple_of(c * chunk + s * 256, 256), 256)
             wide[at, :] = stage[at, :].astype(f32)
 
-    for line in range(CAPACITY // 128):
-
-        @pl.loop(0, 128 // TOGETHER)
+    list_copy.wait()
+    listed[CAPACITY:, :] = jnp.zeros_like(listed[CAPACITY:, :])
+    for line in range(LINES):
+
+        @pl.loop(0, min(128, CAPACITY - 128 * line) // TOGETHER)
         def _(g):
             at = pl.multiple_of(g * TOGETHER, TOGETHER)
             fetched = []
             for q in range(TOGETHER):
-                row = lax.shift_right_logical(slist[line, at + q], 11)
-                fetched.append(wide[pl.ds(row, 1), :])
+                fetched.append(wide[pl.ds(slist[line, at + q], 1), :])
             for q in range(TOGETHER):
                 listed[pl.ds(line * 128 + at + q, 1), :] = fetched[q]
 
@@ -267,12 +289,12 @@
     eye = iota(square, 0) == iota(square, 1)
     ones = jnp.ones(square, bf16)
     picked = listed[...].astype(bf16)
-    wanted = vlist[...] & 2047
+    wanted = vlist[8:, :]
     for b in range(part_ref.shape[0] // 128):
         select = jnp.concatenate(
             [
                 jnp.where(wanted[n : n + 1, :] == iota(square, 0) + (128 * b + 1), f32(1.0), f32(0.0)).astype(bf16)
-                for n in range(CAPACITY // 128)
+                for n in range(LINES)
             ],
             axis=1,
         )
@@ -335,16 +357,16 @@
             copy.start()
             zcopies.append(copy)
     tower(PLAN[2])
+    loads[3].wait()
     for copy in zcopies:
         copy.wait_recv()
     pooled = pooled + recvz[0] + recvz[1] + recvz[2]
 
-    mine_at = pl.ds(pl.multiple_of(table * width, width), width)
     p0 = pooled.astype(bf16)
     rest = pooled - p0.astype(f32)
     p1 = rest.astype(bf16)
     p2 = (rest - p1.astype(f32)).astype(bf16)
-    terms = jnp.dot(jnp.concatenate([p0, p1, p2], axis=0), weight_ref[mine_at, :], preferred_element_type=f32)
+    terms = jnp.dot(jnp.concatenate([p0, p1, p2], axis=0), wv[...], preferred_element_type=f32)
     terms = terms[:per] + terms[per : 2 * per] + terms[2 * per :]
     for b in range(groups):
         sendt[b] = terms[b * own : (b + 1) * own, :]
@@ -384,46 +406,57 @@
                 src_ref=embed_ref,
                 dst_ref=gathered.at[me],
                 send_sem=sg,
-                recv_sem=rg,
+                recv_sem=rg.at[lax.rem(lax.div(zp, 2) + lax.div(zi, 2), 2)],
                 device_id=(zp * NX + xp, cand, lax.rem(dp + n, ndp)),
                 device_id_type=MESH,
             ).start()
 
     gathered[me] = embed
     tower(PLAN[4])
+    lines = place_ref.shape[0]
+    half = ntab * ndp // 2
+
+    def add_scores(side, first):
+        pieces = [gathered[side * half + b] for b in range(half)]
+        items = jnp.concatenate(pieces, axis=0)
+        item_high, item_low = split2(items)
+        count = items.shape[0]
+        stacked = jnp.concatenate([item_high, item_low], axis=0)
+
+        def score(c, _):
+            at = pl.ds(pl.multiple_of(c * USERS_AT_ONCE, USERS_AT_ONCE), USERS_AT_ONCE)
+            both = jnp.dot(stacked, high_ref[:, at], preferred_element_type=f32)
+            rest = jnp.dot(item_high, low_ref[:, at], preferred_element_type=f32)
+            scores = both[:count] + both[count:] + rest
+            sums = jnp.sum(jnp.exp(scores), axis=0, keepdims=True)
+            for h in range(USERS_AT_ONCE // 128):
+                line = c * (USERS_AT_ONCE // 128) + h
+                place = place_ref[pl.ds(line, 1), :]
+                block = lax.shift_right_logical(place, 4)
+                here = lax.rem(block, ncand) == cand
+                row = jnp.where(here, lax.div(block, ncand) * 16 + (place & 15) - side * count, -1)
+                part = scores[:, h * 128 : (h + 1) * 128]
+                positive = jnp.sum(
+                    jnp.where(iota((count, 128), 0) == row, part, f32(0.0)), axis=0, keepdims=True
+                )
+                total = sums[:, h * 128 : (h + 1) * 128]
+                if not first:
+                    total = total + stats[pl.ds(line, 1), :]
+                    positive = positive + stats[pl.ds(line + lines, 1), :]
+                stats[pl.ds(line, 1), :] = total
+                stats[pl.ds(line + lines, 1), :] = positive
+            return 0
+
+        lax.fori_loop(0, high_ref.shape[1] // USERS_AT_ONCE, score, 0, unroll=UNROLL)
+
     most = gathered.at[pl.ds(0, ntab * ndp - 1)]
-    pltpu.make_async_copy(most, most, rg).wait()
-
-    pieces = [gathered[b] for b in range(ntab * ndp)]
-    items = jnp.concatenate(pieces, axis=0)
-    item_high, item_low = split2(items)
-    dims = (((1,), (1,)), ((), ()))
-    count = items.shape[0]
-
-    def score(c, _):
-        at = pl.ds(pl.multiple_of(c * USERS_AT_ONCE, USERS_AT_ONCE), USERS_AT_ONCE)
-        high = high_ref[at, :]
-        scores = (
-            lax.dot_general(item_high, high, dims, preferred_element_type=f32)
-            + lax.dot_general(item_low, high, dims, preferred_element_type=f32)
-            + lax.dot_general(item_high, low_ref[at, :], dims, preferred_element_type=f32)
-        )
-        sums = jnp.sum(jnp.exp(scores), axis=0, keepdims=True)
-        for h in range(USERS_AT_ONCE // 128):
-            line = c * (USERS_AT_ONCE // 128) + h
-            place = place_ref[pl.ds(line, 1), :]
-            block = lax.shift_right_logical(place, 4)
-            here = lax.rem(block, ncand) == cand
-            row = jnp.where(here, lax.div(block, ncand) * 16 + (place & 15), -1)
-            part = scores[:, h * 128 : (h + 1) * 128]
-            positive = jnp.sum(
-                jnp.where(iota((count, 128), 0) == row, part, f32(0.0)), axis=0, keepdims=True
-            )
-            stats[pl.ds(line, 1), :] = sums[:, h * 128 : (h + 1) * 128]
-            stats[pl.ds(line + place_ref.shape[0], 1), :] = positive
-        return 0
-
-    lax.fori_loop(0, xv.shape[0] // USERS_AT_ONCE, score, 0, unroll=4)
+    near = gathered.at[pl.ds(0, half - 1)]
+    far = gathered.at[pl.ds(0, half)]
+    side = lax.div(zi, 2)
+    pltpu.make_async_copy(near, near, rg.at[0]).wait()
+    add_scores(side, True)
+    pltpu.make_async_copy(far, far, rg.at[1]).wait()
+    add_scores(1 - side, False)
 
     scopies = []
     for o in range(1, ncand):
@@ -447,7 +480,6 @@
     for copy in scopies:
         copy.wait_recv()
     both = stats[...] + others[0] + others[1] + others[2]
-    lines = place_ref.shape[0]
     loss_ref[...] = jnp.log(both[:lines]) - both[lines:]
     for copy in scopies:
         copy.wait_send()
@@ -456,7 +488,8 @@
 def step(flat, extra, lengths, table, item_weight, features, user_w1, user_w2, places):
     items, width = extra.shape
     rows = table.shape[0]
-    users, embed = features.shape[0], user_w2.shape[1]
+    users, features_in = features.shape
+    hidden, embed = user_w2.shape
     per = items // (NX * NZ)
     own = per // 16
     lines = users // 128
@@ -467,15 +500,19 @@
         step_kernel,
         name="step",
         out_shape=(jax.ShapeDtypeStruct((own, embed), f32), jax.ShapeDtypeStruct((lines, 128), f32)),
-        in_specs=[pl.BlockSpec(memory_space=pltpu.SMEM), vmem, vmem, vmem, hbm, *[vmem] * 5],
+        in_specs=[vmem, vmem, vmem, hbm, hbm, hbm, hbm, hbm, vmem],
         out_specs=(vmem, vmem),
         scratch_shapes=[
             pltpu.VMEM((rows, width), bf16),
             pltpu.VMEM((rows, width), f32),
-            pltpu.VMEM((CAPACITY, width), f32),
+            pltpu.VMEM((128 * LINES, width), f32),
             pltpu.VMEM((items, width), f32),
-            pltpu.VMEM((users, embed), bf16),
-            pltpu.VMEM((users, embed), bf16),
+            pltpu.VMEM((users, features_in), bf16),
+            pltpu.VMEM((features_in, hidden), bf16),
+            pltpu.VMEM((hidden, embed), bf16),
+            pltpu.VMEM((width, embed), bf16),
+            pltpu.VMEM((embed, users), bf16),
+            pltpu.VMEM((embed, users), bf16),
             pltpu.VMEM((NZ, NX - 1, per, width), f32),
             pltpu.VMEM((NZ - 1, per, width), f32),
             pltpu.VMEM((NZ - 1, per, width), f32),
@@ -485,7 +522,10 @@
             pltpu.VMEM((64, own, embed), f32),
             pltpu.VMEM((2 * lines, 128), f32),
             pltpu.VMEM((3, 2 * lines, 128), f32),
+            pltpu.SMEM((8, 128), i32),
+            dma,
             dma((CHUNKS,)),
+            dma((4,)),
             dma((NZ, NX - 1)),
             dma((NZ, NX - 1)),
             dma((NZ - 1,)),
@@ -493,24 +533,47 @@
             dma,
             dma,
             dma,
-            dma,
+            dma((2,)),
             dma((3,)),
             dma((3,)),
         ],
         compiler_params=pltpu.CompilerParams(
-            collective_id=0, has_side_effects=True, vmem_limit_bytes=46 * 2**20
+            collective_id=0, has_side_effects=True, vmem_limit_bytes=52 * 2**20
         ),
         cost_estimate=pl.CostEstimate(flops=5 * 10**9, bytes_accessed=5 * 2**20, transcendentals=0),
-    )(flat, flat, extra, lengths, table, item_weight, features, user_w1, user_w2, places)
+    )(flat, extra, lengths, table, item_weight, features, user_w1, user_w2, places)
+
+
+def finish_kernel(item_ref, loss_ref, item_out, loss_out):
+    item_out[...] = item_ref[...]
+    loss_out[...] = loss_ref[...]
+
+
+def finish(item_emb, loss):
+    vmem = pl.BlockSpec(memory_space=pltpu.VMEM)
+    return pl.pallas_call(
+        finish_kernel,
+        name="finish",
+        out_shape=(
+            jax.ShapeDtypeStruct(item_emb.shape, f32),
+            jax.ShapeDtypeStruct(loss.shape, f32),
+        ),
+        in_specs=[vmem, vmem],
+        out_specs=(vmem, vmem),
+        compiler_params=pltpu.CompilerParams(vmem_limit_bytes=2**20),
+    )(item_emb, loss)
 
 
 def body(
     tables, bag_ids, bag_lengths, item_weight, user_features, user_w1, user_w2, positive_items
 ):
-    flat, extra = make_list(bag_ids[0].T, bag_lengths, tables[0])
+    ids = bag_ids[0].T
+    ids = jnp.where(iota(ids.shape, 0) < bag_lengths, ids, i32(-1))
+    flat, extra = make_list(ids, tables[0])
     item_emb, loss = step(
         flat, extra, bag_lengths, tables[0], item_weight, user_features, user_w1, user_w2, positive_items.reshape(-1, 128)
     )
+    item_emb, loss = finish(item_emb, loss)
     return (item_emb, loss.reshape(-1))
 
 

time: 50.3 us -> 46.8 us (0.930)
  local copies, waits for them, and re-layouts: 4.17 us -> 0.01 us
  other arithmetic: 0 us -> 0.91 us
    unnamed x16 -> x6, local copies, waits for them, and re-layouts: 4.17 us -> 0.01 us
    pallas_call x1, Pallas kernels: 44.5 us -> 43.5 us  [step(): pl.pallas_call(step_kernel, name='step', out_shape=(jax.ShapeDtypeStruct(...]
    select_n x0 -> x1, other arithmetic: none -> 0.91 us  [body(): ids = jnp.where(iota(ids.shape, 0) < bag_lengths, ids, i32(-1))]
    pallas_call x0 -> x1, Pallas kernels: none -> 0.61 us  [finish(): pl.pallas_call(finish_kernel, name='finish', out_shape=(jax.ShapeDtypeStr...]
where the time goes in v5:
time: 46.8 us; the launch traced here: 46.7 us
  Pallas kernels  45 us (96%)
  other arithmetic  0.91 us (2%)
  between operations  0.7 us (1%)
    pallas_call x1, Pallas kernels, step(): pl.pallas_call(step_kernel, name='step', out_shape=(jax.ShapeDtypeStruct(...  43.5 us
    pallas_call x1, Pallas kernels, make_list(): pl.pallas_call(list_kernel, name='list', out_shape=(jax.ShapeDtypeStruct(...  0.94 us

profile of v5, /device:TPU:1, one launch (start us, length us, event | category | flops | bytes accessed | tf_op | source)
XLA Modules:
  0.0 46.7 jit_solution(2468628695906341978)
XLA Ops:
  0.6 0.0 copy-start
  0.6 0.0 copy-start.2
  0.7 0.0 copy-start.1
  0.7 0.9 %bitcast_select_fusion.ids_ref = s32[16,1024]{1,0:T(8,128)S(1)} fusion(s32[1,1024,16]{1,2,0:T(8,128)} %param.9, s32[1024]{0:T(1024)} %bitcast.8), kind=kLoop, calls=%fused_computation | loop fusion | flops 32768 | bytes 135168 | tf_op jit(solution)/shard_map/jit(_where)/select_n | solution.py:571
  1.6 0.9 %list.1 = (s32[16,128]{1,0:T(8,128)S(1)}, f32[1024,128]{1,0:T(8,128)S(1)}) custom-call(s32[16,1024]{1,0:T(8,128)S(1)} %bitcast_select_fusion.ids_ref, bf16[32768,128]{1,0:T(8,128)(2,1)} %bitcast.10), custom_call_target="tpu_custom_call" | custom-call | flops 100000000 | bytes 1048576 | tf_op jit(solution)/shard_map/list/pallas_call | solution.py:161
  2.5 0.0 copy-done
  2.5 0.0 copy-done.2
  2.5 0.0 copy-done.1
  2.6 43.5 %step.1 = (f32[4,256]{1,0:T(4,128)S(1)}, f32[16,128]{1,0:T(8,128)S(1)}) custom-call(s32[16,128]{1,0:T(8,128)S(1)} %get-tuple-element.8.vlist, f32[1024,128]{1,0:T(8,128)S(1)} %get-tuple-element.9.extra_ref, s32[1,1024]{1,0:T(1,128)S(1)} %copy-done, bf16[32768,128]{1,0:T(8,128)(2,1)} %bitcast.11, bf16[2048,256]{1,0:T(8,128)(2,1)} %weight_ref.1, ...), custom_call_target="tpu_custom_call" | custom-call | flops 5000000000 | bytes 5242880 | tf_op jit(solution)/shard_map/step/pallas_call | solution.py:499
  46.1 0.6 %finish.1 = (f32[4,256]{1,0:T(4,128)}, f32[16,128]{1,0:T(8,128)}) custom-call(f32[4,256]{1,0:T(4,128)S(1)} %get-tuple-element.10.item_ref, f32[16,128]{1,0:T(8,128)S(1)} %get-tuple-element.11.loss_ref), custom_call_target="tpu_custom_call" | custom-call | tf_op jit(solution)/shard_map/finish/pallas_call | solution.py:554
Async XLA Ops:
  0.6 1.9 %copy-start = (s32[1,1024]{1,0:T(1,128)S(1)}, s32[1,1024]{1,0:T(1,128)}, u32[]{:S(2)}) copy-start(s32[1,1024]{1,0:T(1,128)} %len_ref.1) | copy-start | bytes 12292
  0.6 1.9 %copy-start.2 = (s32[2048]{0:T(1024)S(1)}, s32[2048]{0:T(1024)}, u32[]{:S(2)}) copy-start(s32[2048]{0:T(1024)} %param.15) | copy-start | bytes 24580
  0.7 1.9 %copy-start.1 = (bf16[1024,256]{1,0:T(8,128)(2,1)S(1)}, bf16[1024,256]{1,0:T(8,128)(2,1)}, u32[]{:S(2)}) copy-start(bf16[1024,256]{1,0:T(8,128)(2,1)} %w2_ref.1) | copy-start | bytes 1572868

commit v6 on v5

--- a/solution.py
+++ b/solution.py
@@ -39,10 +39,7 @@
     local = ids - base
     live = (local >= 0) & (local < rows)
     item = lax.div(r, positions) * 128 + lane
-    per = items // (NX * NZ)
-    block = lax.div(item, per)
-    dest = (lax.rem(block, NX) * NZ + lax.div(block, NX)) * per + lax.rem(item, per)
-    code = local * 2048 + dest + 1
+    code = local * 2048 + item + 1
     below = jnp.where(iota((slots, slots), 0) >= iota((slots, slots), 1), f32(1.0), f32(0.0)).astype(bf16)
     ones = jnp.ones((128, 128), bf16)
 
@@ -196,7 +193,7 @@
 
 
 def step_kernel(vlist, extra_ref, len_ref, table_ref, weight_ref, x_ref, w1_ref, w2_ref, place_ref, item_ref, loss_ref,
-                stage, wide, listed, part_ref, xv, w1v, w2v, wv, high_ref, low_ref, recvx, sendz, recvz, sendt, recvt, embed_ref,
+                stage, wide, listed, part_ref, columns, xv, w1v, w2v, wv, high_ref, low_ref, recvx, sendz, recvz, sendt, recvt, embed_ref,
                 gathered, stats, others, slist, list_sem, table_sems, load_sems, sx, rx, sz, rz, st, rt, sg, rg, ss, rs):
     tab, cand, dp = lax.axis_index("tab"), lax.axis_index("cand"), lax.axis_index("dp")
     xi, zi = lax.rem(tab, NX), lax.div(tab, NX)
@@ -261,6 +258,14 @@
             high_ref[:, at] = high
             low_ref[:, at] = low
 
+    square = (128, 128)
+    eye = iota(square, 0) == iota(square, 1)
+    for b in range(part_ref.shape[0] // 128):
+        spread = jnp.broadcast_to(len_ref[:, 128 * b : 128 * (b + 1)].astype(f32), square)
+        columns[128 * b : 128 * (b + 1), :] = jnp.dot(
+            jnp.where(eye, spread, f32(0.0)).astype(bf16), jnp.ones(square, bf16), preferred_element_type=f32
+        )
+
     for c in range(CHUNKS):
         table_loads[c].wait()
         if c == CHUNKS - 2:
@@ -285,43 +290,30 @@
             for q in range(TOGETHER):
                 listed[pl.ds(line * 128 + at + q, 1), :] = fetched[q]
 
-    square = (128, 128)
-    eye = iota(square, 0) == iota(square, 1)
-    ones = jnp.ones(square, bf16)
+    pl.semaphore_wait(barrier, groups - 1 + NZ - 1 + NX - 1)
     picked = listed[...].astype(bf16)
     wanted = vlist[8:, :]
-    for b in range(part_ref.shape[0] // 128):
-        select = jnp.concatenate(
-            [
-                jnp.where(wanted[n : n + 1, :] == iota(square, 0) + (128 * b + 1), f32(1.0), f32(0.0)).astype(bf16)
-                for n in range(LINES)
-            ],
-            axis=1,
-        )
-        ends = []
-        for h in range(128 // per):
-            to = b * (128 // per) + h
-            t = (to % NZ) * NX + to // NZ
-            ends.append(len_ref[:, t * per : (t + 1) * per])
-        spread = jnp.broadcast_to(jnp.concatenate(ends, axis=1).astype(f32), square)
-        column = jnp.dot(jnp.where(eye, spread, f32(0.0)).astype(bf16), ones, preferred_element_type=f32)
-        at = pl.ds(128 * b, 128)
-        part_ref[at, :] = (jnp.dot(select, picked, preferred_element_type=f32) + extra_ref[at, :]) / column
-
-    if PLAN[0]:
-        tower(PLAN[0])
-    pl.semaphore_wait(barrier, groups - 1 + NZ - 1 + NX - 1)
-
+    turns = (3, 2, 1, 0)
+    beside = {3: 3 - zi, 2: lax.rem(zi + 2, NZ), 1: zi + 1 - 2 * lax.rem(zi, 2), 0: zi}
     xcopies = []
-    turns = (2, 1, 3, 0)
     for n, k in enumerate(turns):
-        zp = lax.rem(zi + k, NZ)
+        zp = beside[k]
+        for h in range(NX * per // 128):
+            start = pl.multiple_of(zp * (NX * per) + 128 * h, 128)
+            select = jnp.concatenate(
+                [
+                    jnp.where(wanted[line : line + 1, :] == iota(square, 0) + (start + 1), f32(1.0), f32(0.0)).astype(bf16)
+                    for line in range(LINES)
+                ],
+                axis=1,
+            )
+            at = pl.ds(start, 128)
+            part_ref[at, :] = (jnp.dot(select, picked, preferred_element_type=f32) + extra_ref[at, :]) / columns[at, :]
         row = []
-        for o in range(1, NX):
+        for o in (2, 1, 3):
             xp = lax.rem(xi + o, NX)
-            src = part_ref.at[pl.ds(pl.multiple_of((xp * NZ + zp) * per, per), per)]
             copy = pltpu.make_async_remote_copy(
-                src_ref=src,
+                src_ref=part_ref.at[pl.ds(pl.multiple_of((zp * NX + xp) * per, per), per)],
                 dst_ref=recvx.at[n, o - 1],
                 send_sem=sx.at[n, o - 1],
                 recv_sem=rx.at[n, o - 1],
@@ -337,10 +329,10 @@
     zcopies = []
     pooled = None
     for n, k in enumerate(turns):
-        zp = lax.rem(zi + k, NZ)
+        zp = beside[k]
         for copy in xcopies[n]:
             copy.wait_recv()
-        mine = part_ref[pl.ds(pl.multiple_of((xi * NZ + zp) * per, per), per), :]
+        mine = part_ref[pl.ds(pl.multiple_of((zp * NX + xi) * per, per), per), :]
         total = mine + recvx[n, 0] + recvx[n, 1] + recvx[n, 2]
         if k == 0:
             pooled = total
@@ -396,18 +388,24 @@
 
     me = tab * ndp + dp
 
-    for k in turns:
-
-        @pl.loop(0 if k else 1, NX * ndp)
+    ring = 2 * NZ
+    core = lax.rem(cand, 2)
+    zring = lax.div(cand, 2) * NZ + zi
+    for away in (2 + 4 * core, 1, ring - 1, 0):
+        zq = lax.rem(zring + away, ring)
+        zp = lax.rem(zq, NZ)
+        share = lax.div(zq, NZ) * 2 + core
+        same = isinstance(away, int) and away == 0
+
+        @pl.loop(1 if same else 0, NX * ndp, unroll=5 if same else 4)
         def _(n):
-            zp = lax.rem(zi + k, NZ)
             xp = lax.rem(xi + lax.div(n, ndp), NX)
             pltpu.make_async_remote_copy(
                 src_ref=embed_ref,
                 dst_ref=gathered.at[me],
                 send_sem=sg,
                 recv_sem=rg.at[lax.rem(lax.div(zp, 2) + lax.div(zi, 2), 2)],
-                device_id=(zp * NX + xp, cand, lax.rem(dp + n, ndp)),
+                device_id=(zp * NX + xp, share, lax.rem(dp + n, ndp)),
                 device_id_type=MESH,
             ).start()
 
@@ -433,7 +431,10 @@
                 line = c * (USERS_AT_ONCE // 128) + h
                 place = place_ref[pl.ds(line, 1), :]
                 block = lax.shift_right_logical(place, 4)
-                here = lax.rem(block, ncand) == cand
+                apart = (lax.shift_right_logical(block, 4) - zi) & (NZ - 1)
+                apart = jnp.where(apart == 3, ring - 1, jnp.where(apart == 2, 6 - 4 * core, apart))
+                from_z = (zring + apart) & (ring - 1)
+                here = (block & 3) == lax.shift_right_logical(from_z, 2) * 2 + core
                 row = jnp.where(here, lax.div(block, ncand) * 16 + (place & 15) - side * count, -1)
                 part = scores[:, h * 128 : (h + 1) * 128]
                 positive = jnp.sum(
@@ -506,6 +507,7 @@
             pltpu.VMEM((rows, width), bf16),
             pltpu.VMEM((rows, width), f32),
             pltpu.VMEM((128 * LINES, width), f32),
+            pltpu.VMEM((items, width), f32),
             pltpu.VMEM((items, width), f32),
             pltpu.VMEM((users, features_in), bf16),
             pltpu.VMEM((features_in, hidden), bf16),

time: 46.8 us -> 45.9 us (0.981)
  Pallas kernels: 45 us -> 44.2 us
    pallas_call x1, Pallas kernels: 43.5 us -> 42.7 us  [step(): pl.pallas_call(step_kernel, name='step', out_shape=(jax.ShapeDtypeStruct(...]
where the time goes in v6:
time: 45.9 us; the launch traced here: 45.8 us
  Pallas kernels  44.2 us (96%)
  other arithmetic  0.91 us (2%)
  between operations  0.7 us (2%)
    pallas_call x1, Pallas kernels, step(): pl.pallas_call(step_kernel, name='step', out_shape=(jax.ShapeDtypeStruct(...  42.7 us

profile of v6, /device:TPU:1, one launch (start us, length us, event | category | flops | bytes accessed | tf_op | source)
XLA Modules:
  0.0 45.8 jit_solution(14328169059379970308)
XLA Ops:
  0.6 0.0 copy-start
  0.6 0.0 copy-start.2
  0.7 0.0 copy-start.1
  0.7 0.9 %bitcast_select_fusion.ids_ref = s32[16,1024]{1,0:T(8,128)S(1)} fusion(s32[1,1024,16]{1,2,0:T(8,128)} %param.9, s32[1024]{0:T(1024)} %bitcast.8), kind=kLoop, calls=%fused_computation | loop fusion | flops 32768 | bytes 135168 | tf_op jit(solution)/shard_map/jit(_where)/select_n | solution.py:573
  1.6 0.9 %list.1 = (s32[16,128]{1,0:T(8,128)S(1)}, f32[1024,128]{1,0:T(8,128)S(1)}) custom-call(s32[16,1024]{1,0:T(8,128)S(1)} %bitcast_select_fusion.ids_ref, bf16[32768,128]{1,0:T(8,128)(2,1)} %bitcast.10), custom_call_target="tpu_custom_call" | custom-call | flops 100000000 | bytes 1048576 | tf_op jit(solution)/shard_map/list/pallas_call | solution.py:158
  2.5 0.0 copy-done
  2.5 0.0 copy-done.2
  2.5 0.0 copy-done.1
  2.5 42.7 %step.1 = (f32[4,256]{1,0:T(4,128)S(1)}, f32[16,128]{1,0:T(8,128)S(1)}) custom-call(s32[16,128]{1,0:T(8,128)S(1)} %get-tuple-element.8.vlist, f32[1024,128]{1,0:T(8,128)S(1)} %get-tuple-element.9.extra_ref, s32[1,1024]{1,0:T(1,128)S(1)} %copy-done, bf16[32768,128]{1,0:T(8,128)(2,1)} %bitcast.11, bf16[2048,256]{1,0:T(8,128)(2,1)} %weight_ref.1, ...), custom_call_target="tpu_custom_call" | custom-call | flops 5000000000 | bytes 5242880 | tf_op jit(solution)/shard_map/step/pallas_call | solution.py:500
  45.2 0.6 %finish.1 = (f32[4,256]{1,0:T(4,128)}, f32[16,128]{1,0:T(8,128)}) custom-call(f32[4,256]{1,0:T(4,128)S(1)} %get-tuple-element.10.item_ref, f32[16,128]{1,0:T(8,128)S(1)} %get-tuple-element.11.loss_ref), custom_call_target="tpu_custom_call" | custom-call | tf_op jit(solution)/shard_map/finish/pallas_call | solution.py:556
Async XLA Ops:
  0.6 1.9 %copy-start = (s32[1,1024]{1,0:T(1,128)S(1)}, s32[1,1024]{1,0:T(1,128)}, u32[]{:S(2)}) copy-start(s32[1,1024]{1,0:T(1,128)} %len_ref.1) | copy-start | bytes 12292
  0.6 1.9 %copy-start.2 = (s32[2048]{0:T(1024)S(1)}, s32[2048]{0:T(1024)}, u32[]{:S(2)}) copy-start(s32[2048]{0:T(1024)} %param.15) | copy-start | bytes 24580
  0.7 1.9 %copy-start.1 = (bf16[1024,256]{1,0:T(8,128)(2,1)S(1)}, bf16[1024,256]{1,0:T(8,128)(2,1)}, u32[]{:S(2)}) copy-start(bf16[1024,256]{1,0:T(8,128)(2,1)} %w2_ref.1) | copy-start | bytes 1572868

commit v7 on v6

--- a/solution.py
+++ b/solution.py
@@ -16,7 +16,7 @@
 CHUNKS = 8
 CAPACITY = 704
 LINES = 6
-LANE_DEPTH = 20
+LANE_DEPTH = 24
 
 
 def iota(shape, dim):
@@ -230,11 +230,14 @@
     def greet(device):
         pl.semaphore_signal(barrier, inc=1, device_id=device, device_id_type=MESH)
 
-    for a in (2, 3, 1, 0):
-        for k in (2, 1, 3, 0):
-            if a or k:
-                greet((tab, lax.rem(cand + a, ncand), lax.rem(dp + k, ndp)))
-    for k in range(1, NZ):
+    ring = 2 * NZ
+    core = lax.rem(cand, 2)
+    zring = lax.div(cand, 2) * NZ + zi
+    opposite = lax.rem(zi + 2, NZ) * NX + xi
+    for k in (2, 1, 3, 0):
+        for a in range(ncand):
+            greet((opposite, a, lax.rem(dp + k, ndp)))
+    for k in (1, 3):
         greet((lax.rem(zi + k, NZ) * NX + xi, cand, dp))
     for k in range(1, NX):
         greet((zi * NX + lax.rem(xi + k, NX), cand, dp))
@@ -290,7 +293,7 @@
             for q in range(TOGETHER):
                 listed[pl.ds(line * 128 + at + q, 1), :] = fetched[q]
 
-    pl.semaphore_wait(barrier, groups - 1 + NZ - 1 + NX - 1)
+    pl.semaphore_wait(barrier, groups + NZ - 2 + NX - 1)
     picked = listed[...].astype(bf16)
     wanted = vlist[8:, :]
     turns = (3, 2, 1, 0)
@@ -363,34 +366,30 @@
     for b in range(groups):
         sendt[b] = terms[b * own : (b + 1) * own, :]
 
-    for a in (2, 3, 1, 0):
-        for k in (2, 1, 3, 0):
-            if a or k:
-                there, that = lax.rem(cand + a, ncand), lax.rem(dp + k, ndp)
-                pltpu.make_async_remote_copy(
-                    src_ref=sendt.at[there * ndp + that],
-                    dst_ref=recvt.at[a * ndp + k - 1],
-                    send_sem=st,
-                    recv_sem=rt,
-                    device_id=(tab, there, that),
-                    device_id_type=MESH,
-                ).start()
+    for k in (2, 1, 3, 0):
+        for a in range(ncand):
+            that = lax.rem(dp + k, ndp)
+            holder = lax.rem((a // 2) * NZ + zi + (2 if a % 2 else ring - 2), ring)
+            pltpu.make_async_remote_copy(
+                src_ref=sendt.at[a * ndp + that],
+                dst_ref=recvt.at[table],
+                send_sem=st,
+                recv_sem=rt,
+                device_id=(opposite, lax.div(holder, NZ) * 2 + a % 2, that),
+                device_id_type=MESH,
+            ).start()
 
     tower(PLAN[3])
     all_t = pltpu.make_async_copy(recvt, recvt, rt)
     all_t.wait()
-    total = sendt[table]
-    for b in range(groups - 1):
+    total = recvt[0]
+    for b in range(1, groups):
         total = total + recvt[b]
     embed = unit_rows(total)
     embed_ref[...] = embed
-    item_ref[...] = embed
 
     me = tab * ndp + dp
 
-    ring = 2 * NZ
-    core = lax.rem(cand, 2)
-    zring = lax.div(cand, 2) * NZ + zi
     for away in (2 + 4 * core, 1, ring - 1, 0):
         zq = lax.rem(zring + away, ring)
         zp = lax.rem(zq, NZ)
@@ -431,11 +430,12 @@
                 line = c * (USERS_AT_ONCE // 128) + h
                 place = place_ref[pl.ds(line, 1), :]
                 block = lax.shift_right_logical(place, 4)
-                apart = (lax.shift_right_logical(block, 4) - zi) & (NZ - 1)
+                apart = (lax.shift_right_logical(block, 4) + 2 - zi) & (NZ - 1)
                 apart = jnp.where(apart == 3, ring - 1, jnp.where(apart == 2, 6 - 4 * core, apart))
-                from_z = (zring + apart) & (ring - 1)
-                here = (block & 3) == lax.shift_right_logical(from_z, 2) * 2 + core
-                row = jnp.where(here, lax.div(block, ncand) * 16 + (place & 15) - side * count, -1)
+                owner = (zring + apart + 2 + 4 * core) & (ring - 1)
+                here = (block & 3) == lax.shift_right_logical(owner, 2) * 2 + core
+                slot = (lax.shift_right_logical(block, 2) + 2 * NX) & (ntab - 1)
+                row = jnp.where(here, slot * 16 + (place & 15) - side * count, -1)
                 part = scores[:, h * 128 : (h + 1) * 128]
                 positive = jnp.sum(
                     jnp.where(iota((count, 128), 0) == row, part, f32(0.0)), axis=0, keepdims=True
@@ -457,6 +457,7 @@
     pltpu.make_async_copy(near, near, rg.at[0]).wait()
     add_scores(side, True)
     pltpu.make_async_copy(far, far, rg.at[1]).wait()
+    item_ref[...] = gathered[opposite * ndp + dp]
     add_scores(1 - side, False)
 
     scopies = []
@@ -519,7 +520,7 @@
             pltpu.VMEM((NZ - 1, per, width), f32),
             pltpu.VMEM((NZ - 1, per, width), f32),
             pltpu.VMEM((16, own, embed), f32),
-            pltpu.VMEM((15, own, embed), f32),
+            pltpu.VMEM((16, own, embed), f32),
             pltpu.VMEM((own, embed), f32),
             pltpu.VMEM((64, own, embed), f32),
             pltpu.VMEM((2 * lines, 128), f32),

time: 45.9 us -> 45.2 us (0.985)
  Pallas kernels: 44.2 us -> 43.5 us
    pallas_call x1, Pallas kernels: 42.7 us -> 41.9 us  [step(): pl.pallas_call(step_kernel, name='step', out_shape=(jax.ShapeDtypeStruct(...]
where the time goes in v7:
time: 45.2 us; the launch traced here: 45.1 us
  Pallas kernels  43.5 us (96%)
  other arithmetic  0.91 us (2%)
  between operations  0.7 us (2%)
    pallas_call x1, Pallas kernels, step(): pl.pallas_call(step_kernel, name='step', out_shape=(jax.ShapeDtypeStruct(...  41.9 us
    pallas_call x1, Pallas kernels, make_list(): pl.pallas_call(list_kernel, name='list', out_shape=(jax.ShapeDtypeStruct(...  1.01 us
    select_n x1, other arithmetic, body(): ids = jnp.where(iota(ids.shape, 0) < bag_lengths, ids, i32(-1))  0.91 us

profile of v7, /device:TPU:1, one launch (start us, length us, event | category | flops | bytes accessed | tf_op | source)
XLA Modules:
  0.0 45.1 jit_solution(6798128610495338833)
XLA Ops:
  0.6 0.0 copy-start
  0.6 0.0 copy-start.2
  0.7 0.0 copy-start.1
  0.7 0.9 %bitcast_select_fusion.ids_ref = s32[16,1024]{1,0:T(8,128)S(1)} fusion(s32[1,1024,16]{1,2,0:T(8,128)} %param.9, s32[1024]{0:T(1024)} %bitcast.8), kind=kLoop, calls=%fused_computation | loop fusion | flops 32768 | bytes 135168 | tf_op jit(solution)/shard_map/jit(_where)/select_n | solution.py:574
  1.6 1.0 %list.1 = (s32[16,128]{1,0:T(8,128)S(1)}, f32[1024,128]{1,0:T(8,128)S(1)}) custom-call(s32[16,1024]{1,0:T(8,128)S(1)} %bitcast_select_fusion.ids_ref, bf16[32768,128]{1,0:T(8,128)(2,1)} %bitcast.10), custom_call_target="tpu_custom_call" | custom-call | flops 100000000 | bytes 1048576 | tf_op jit(solution)/shard_map/list/pallas_call | solution.py:158
  2.6 0.0 copy-done
  2.6 0.0 copy-done.2
  2.6 0.0 copy-done.1
  2.6 41.9 %step.1 = (f32[4,256]{1,0:T(4,128)S(1)}, f32[16,128]{1,0:T(8,128)S(1)}) custom-call(s32[16,128]{1,0:T(8,128)S(1)} %get-tuple-element.8.vlist, f32[1024,128]{1,0:T(8,128)S(1)} %get-tuple-element.9.extra_ref, s32[1,1024]{1,0:T(1,128)S(1)} %copy-done, bf16[32768,128]{1,0:T(8,128)(2,1)} %bitcast.11, bf16[2048,256]{1,0:T(8,128)(2,1)} %weight_ref.1, ...), custom_call_target="tpu_custom_call" | custom-call | flops 5000000000 | bytes 5242880 | tf_op jit(solution)/shard_map/step/pallas_call | solution.py:501
  44.5 0.6 %finish.1 = (f32[4,256]{1,0:T(4,128)}, f32[16,128]{1,0:T(8,128)}) custom-call(f32[4,256]{1,0:T(4,128)S(1)} %get-tuple-element.10.item_ref, f32[16,128]{1,0:T(8,128)S(1)} %get-tuple-element.11.loss_ref), custom_call_target="tpu_custom_call" | custom-call | tf_op jit(solution)/shard_map/finish/pallas_call | solution.py:557
Async XLA Ops:
  0.6 2.0 %copy-start = (s32[1,1024]{1,0:T(1,128)S(1)}, s32[1,1024]{1,0:T(1,128)}, u32[]{:S(2)}) copy-start(s32[1,1024]{1,0:T(1,128)} %len_ref.1) | copy-start | bytes 12292
  0.6 2.0 %copy-start.2 = (s32[2048]{0:T(1024)S(1)}, s32[2048]{0:T(1024)}, u32[]{:S(2)}) copy-start(s32[2048]{0:T(1024)} %param.15) | copy-start | bytes 24580
  0.7 2.0 %copy-start.1 = (bf16[1024,256]{1,0:T(8,128)(2,1)S(1)}, bf16[1024,256]{1,0:T(8,128)(2,1)}, u32[]{:S(2)}) copy-start(bf16[1024,256]{1,0:T(8,128)(2,1)} %w2_ref.1) | copy-start | bytes 1572868

commit v8 on v7

--- a/solution.py
+++ b/solution.py
@@ -186,7 +186,7 @@
     return v * lax.rsqrt(jnp.mean(v * v, axis=-1, keepdims=True) + epsilon)
 
 
-PLAN = (0, 3, 1, 1, 3)
+PLAN = (0, 3, 0, 2, 3)
 USERS_AT_ONCE = 256
 TOGETHER = 16
 UNROLL = 4
@@ -351,7 +351,8 @@
             )
             copy.start()
             zcopies.append(copy)
-    tower(PLAN[2])
+    if PLAN[2]:
+        tower(PLAN[2])
     loads[3].wait()
     for copy in zcopies:
         copy.wait_recv()

time: 45.2 us -> 45.2 us (level)
  no operation moved by 1% of the time
where the time goes in v8:
time: 45.2 us; the launch traced here: 45.1 us
  Pallas kernels  43.5 us (96%)
  other arithmetic  0.91 us (2%)
  between operations  0.7 us (2%)
    pallas_call x1, Pallas kernels, step(): pl.pallas_call(step_kernel, name='step', out_shape=(jax.ShapeDtypeStruct(...  41.9 us
    pallas_call x1, Pallas kernels, make_list(): pl.pallas_call(list_kernel, name='list', out_shape=(jax.ShapeDtypeStruct(...  1.01 us
    select_n x1, other arithmetic, body(): ids = jnp.where(iota(ids.shape, 0) < bag_lengths, ids, i32(-1))  0.91 us

profile of v8, /device:TPU:1, one launch (start us, length us, event | category | flops | bytes accessed | tf_op | source)
XLA Modules:
  0.0 45.1 jit_solution(9702186315704322608)
XLA Ops:
  0.6 0.0 copy-start
  0.6 0.0 copy-start.2
  0.7 0.0 copy-start.1
  0.7 0.9 %bitcast_select_fusion.ids_ref = s32[16,1024]{1,0:T(8,128)S(1)} fusion(s32[1,1024,16]{1,2,0:T(8,128)} %param.9, s32[1024]{0:T(1024)} %bitcast.8), kind=kLoop, calls=%fused_computation | loop fusion | flops 32768 | bytes 135168 | tf_op jit(solution)/shard_map/jit(_where)/select_n | solution.py:575
  1.6 1.0 %list.1 = (s32[16,128]{1,0:T(8,128)S(1)}, f32[1024,128]{1,0:T(8,128)S(1)}) custom-call(s32[16,1024]{1,0:T(8,128)S(1)} %bitcast_select_fusion.ids_ref, bf16[32768,128]{1,0:T(8,128)(2,1)} %bitcast.10), custom_call_target="tpu_custom_call" | custom-call | flops 100000000 | bytes 1048576 | tf_op jit(solution)/shard_map/list/pallas_call | solution.py:158
  2.6 0.0 copy-done
  2.6 0.0 copy-done.2
  2.6 0.0 copy-done.1
  2.6 41.9 %step.1 = (f32[4,256]{1,0:T(4,128)S(1)}, f32[16,128]{1,0:T(8,128)S(1)}) custom-call(s32[16,128]{1,0:T(8,128)S(1)} %get-tuple-element.8.vlist, f32[1024,128]{1,0:T(8,128)S(1)} %get-tuple-element.9.extra_ref, s32[1,1024]{1,0:T(1,128)S(1)} %copy-done, bf16[32768,128]{1,0:T(8,128)(2,1)} %bitcast.11, bf16[2048,256]{1,0:T(8,128)(2,1)} %weight_ref.1, ...), custom_call_target="tpu_custom_call" | custom-call | flops 5000000000 | bytes 5242880 | tf_op jit(solution)/shard_map/step/pallas_call | solution.py:502
  44.5 0.6 %finish.1 = (f32[4,256]{1,0:T(4,128)}, f32[16,128]{1,0:T(8,128)}) custom-call(f32[4,256]{1,0:T(4,128)S(1)} %get-tuple-element.10.item_ref, f32[16,128]{1,0:T(8,128)S(1)} %get-tuple-element.11.loss_ref), custom_call_target="tpu_custom_call" | custom-call | tf_op jit(solution)/shard_map/finish/pallas_call | solution.py:558
Async XLA Ops:
  0.6 2.0 %copy-start = (s32[1,1024]{1,0:T(1,128)S(1)}, s32[1,1024]{1,0:T(1,128)}, u32[]{:S(2)}) copy-start(s32[1,1024]{1,0:T(1,128)} %len_ref.1) | copy-start | bytes 12292
  0.6 2.0 %copy-start.2 = (s32[2048]{0:T(1024)S(1)}, s32[2048]{0:T(1024)}, u32[]{:S(2)}) copy-start(s32[2048]{0:T(1024)} %param.15) | copy-start | bytes 24580
  0.7 2.0 %copy-start.1 = (bf16[1024,256]{1,0:T(8,128)(2,1)S(1)}, bf16[1024,256]{1,0:T(8,128)(2,1)}, u32[]{:S(2)}) copy-start(bf16[1024,256]{1,0:T(8,128)(2,1)} %w2_ref.1) | copy-start | bytes 1572868
